TPU v7x, 1024 devices: a whole 4x8x16 slice. The times are simulated.
1024 devices in a mesh: gz: 32 (over z_hi, y), gy: 4 (over x), gx: 8 (over z_lo, core).
Axes of the slice: x: 4, y: 8, z: 16 (z_hi: 4, z_lo: 4; z = z_hi * 4 + z_lo), core: 2. Of those that a mesh axis runs over, the one named last changes fastest.
Arguments:
- positions: float32 [3, 8, 8, 256, 128], P(None, 'gx', 'gy', 'gz'), may hold values from 0 to 1
- counts: int32 [8, 8, 256], P('gx', 'gy', 'gz'), may hold values from 104 to 128
Outputs:
- energy: float32 [8, 8, 256, 128], P('gx', 'gy', 'gz')
- forces: float32 [3, 8, 8, 256, 128], P(None, 'gx', 'gy', 'gz')
Inputs may be any that keep to these rules, and one draw needn't show every extreme that they name: `counts`: slot k of a cell holds an atom exactly when k < its count; positions of other slots are not used.
All inputs are finite; a program needn't handle non-finite values.
Results may differ from a plain program's by a relative error of at most 0.0003.
Values sent between devices are 32-bit elements; how exact they have to be, the bound alone decides.
No kernel may reach another device: no remote copies, remote signals or barrier semaphores. Data moves between devices by JAX's collectives and lax.ppermute only.
A program may use at most 32 MiB of HBM per device.

v0:
```python
import jax
import jax.numpy as jnp
from jax import lax
from jax.sharding import PartitionSpec as P

SENTINEL = 4.0
PAIR_SCALE = 0.02
EMBED_SCALE = 0.2
CUTOFF_SQUARED = 0.25
FORCE_SCALE = 8.0
neighbour_offsets = [
    (step_x, step_y, step_z)
    for step_x in (-1, 0, 1)
    for step_y in (-1, 0, 1)
    for step_z in (-1, 0, 1)
]


def with_halo(block, sides, width):
    for axis, dim in sides:
        count = lax.axis_size(axis)
        forward = [(i, i + 1) for i in range(count - 1)]
        forward.append((count - 1, 0))
        backward = [(target, source) for source, target in forward]
        low = lax.ppermute(
            lax.slice_in_dim(block, block.shape[dim] - width, None, axis=dim), axis, forward
        )
        high = lax.ppermute(lax.slice_in_dim(block, 0, width, axis=dim), axis, backward)
        block = jnp.concatenate([low, block, high], axis=dim)
    return block


def pair_geometry(own_cells, far_cells, offset):
    deltas = []
    for component in range(3):
        deltas.append(
            far_cells[component][..., None, :]
            - own_cells[component][..., :, None]
            + offset[component]
        )
    return deltas


def density_terms(own_cells, far_cells, offset, itself):
    deltas = pair_geometry(own_cells, far_cells, offset)
    squared = deltas[0] * deltas[0] + deltas[1] * deltas[1] + deltas[2] * deltas[2]
    weight = jnp.maximum(1.0 - squared / CUTOFF_SQUARED, 0.0)
    square = weight * weight
    if itself:
        slot_count = own_cells.shape[-1]
        square = jnp.where(jnp.eye(slot_count, dtype=bool), 0.0, square)
    return (jnp.sum(square, -1), jnp.sum(PAIR_SCALE * (square * square - 2.0 * square), -1))


def force_terms(own_cells, far_cells, own_fp, far_fp, offset):
    deltas = pair_geometry(own_cells, far_cells, offset)
    squared = deltas[0] * deltas[0] + deltas[1] * deltas[1] + deltas[2] * deltas[2]
    weight = jnp.maximum(1.0 - squared / CUTOFF_SQUARED, 0.0)
    factor = (own_fp[..., :, None] + far_fp[..., None, :]) * (
        -2.0 * weight
    ) + 4.0 * PAIR_SCALE * weight * (1.0 - weight * weight)
    return jnp.stack([FORCE_SCALE * jnp.sum(factor * delta, -1) for delta in deltas])


def settle(stacked, layers):
    lower_rim = stacked[:, :, :, 0:1]
    upper_rim = stacked[:, :, :, layers + 1 : layers + 2]
    both_rims = jnp.concatenate([lower_rim, upper_rim], axis=3)
    returned = with_halo(both_rims, (("gz", 3),), 1)
    interior = stacked[:, :, :, 1 : layers + 1]
    interior = interior.at[:, :, :, 0].add(returned[:, :, :, 0])
    interior = interior.at[:, :, :, layers - 1].add(returned[:, :, :, 3])
    return interior


def per_device(positions, counts):
    slot_count = positions.shape[-1]
    across = positions.shape[1]
    breadth = positions.shape[2]
    layers = positions.shape[3]
    occupied = jnp.arange(slot_count, dtype=jnp.int32) < counts[..., None]
    seated = jnp.where(occupied[None], positions, SENTINEL)
    tower_block = with_halo(seated, (("gz", 3),), 1)
    plate_block = with_halo(seated, (("gy", 2), ("gx", 1)), 1)
    totals = jnp.zeros((2, across, breadth, layers + 2, slot_count), jnp.float32)
    for step_x, step_y, step_z in neighbour_offsets:
        own_cells = tower_block[:, :, :, 1 + step_z : 1 + step_z + layers]
        far_cells = plate_block[
            :, 1 + step_x : 1 + step_x + across, 1 + step_y : 1 + step_y + breadth
        ]
        itself = step_x == 0 and step_y == 0 and (step_z == 0)
        rho_part, pair_part = density_terms(own_cells, far_cells, (step_x, step_y, -step_z), itself)
        totals = totals.at[:, :, :, 1 + step_z : 1 + step_z + layers].add(
            jnp.stack([rho_part, pair_part])
        )
    density = settle(totals, layers)
    rho_sum = density[0]
    pair_sum = density[1]
    fprime = -0.5 * EMBED_SCALE * lax.rsqrt(rho_sum + 1.0)
    carried = jnp.concatenate([seated, fprime[None]], axis=0)
    tower_all = with_halo(carried, (("gz", 3),), 1)
    plate_all = with_halo(carried, (("gy", 2), ("gx", 1)), 1)
    tower_pos = tower_all[:3]
    tower_fp = tower_all[3]
    plate_pos = plate_all[:3]
    plate_fp = plate_all[3]
    pushes = jnp.zeros((3, across, breadth, layers + 2, slot_count), jnp.float32)
    for step_x, step_y, step_z in neighbour_offsets:
        own_cells = tower_pos[:, :, :, 1 + step_z : 1 + step_z + layers]
        far_cells = plate_pos[
            :, 1 + step_x : 1 + step_x + across, 1 + step_y : 1 + step_y + breadth
        ]
        own_fp = tower_fp[:, :, 1 + step_z : 1 + step_z + layers]
        far_fp = plate_fp[1 + step_x : 1 + step_x + across, 1 + step_y : 1 + step_y + breadth]
        pushes = pushes.at[:, :, :, 1 + step_z : 1 + step_z + layers].add(
            force_terms(own_cells, far_cells, own_fp, far_fp, (step_x, step_y, -step_z))
        )
    forces = settle(pushes, layers)
    energy = jnp.where(occupied, -EMBED_SCALE * jnp.sqrt(rho_sum + 1.0) + 0.5 * pair_sum, 0.0)
    forces = jnp.where(occupied[None], forces, 0.0)
    return (energy, forces)


def solution(mesh):
    placed = (P(None, "gx", "gy", "gz", None), P("gx", "gy", "gz"))
    return jax.shard_map(
        per_device,
        mesh=mesh,
        in_specs=placed,
        out_specs=(P("gx", "gy", "gz", None), P(None, "gx", "gy", "gz", None)),
        check_vma=False,
    )
```

profile of v0, /device:TPU:6, one launch (start us, length us, event | category | flops | bytes accessed | tf_op | source)
XLA Modules:
  0.0 189.1 jit_solution(1284886064423162300)
XLA Ops:
  0.6 0.7 copy-done
  1.4 0.7 broadcast_select_fusion.1
  2.1 2.7 %collective-permute-start.1 = (f32[3,1,1,8,128]{4,3,2,1,0:T(8,128)S(1)}, f32[3,1,1,8,128]{4,3,2,1,0:T(8,128)S(1)}, u32[]{:S(2)}, u32[]{:S(2)}) collective-permute-start(f32[3,1,1,8,128]{4,3,2,1,0:T(8,128)S(1)} %get-tuple-element.1025), channel_id=1, source_target_pairs={{8,0},{16,8},{24,16},{0,24},{9,1},{17,9},{25,17},{1,25},{10,2},{18... | collective-permute-start | bytes 36872 | tf_op jit(solution)/shard_map/ppermute | solution.py:28
  4.9 14.2 %collective-permute-start = (f32[3,1,1,8,128]{4,3,2,1,0:T(8,128)S(1)}, f32[3,1,1,8,128]{4,3,2,1,0:T(8,128)S(1)}, u32[]{:S(2)}, u32[]{:S(2)}) collective-permute-start(f32[3,1,1,8,128]{4,3,2,1,0:T(8,128)S(1)} %get-tuple-element.1026), channel_id=1, source_target_pairs={{0,8},{8,16},{16,24},{24,0},{1,9},{9,17},{17,25},{25,1},{2,10},{10... | collective-permute-start | bytes 36872 | tf_op jit(solution)/shard_map/ppermute | solution.py:25
  19.1 1.9 %collective-permute-start.3 = (f32[3,1,2,1,128]{4,3,2,1,0:T(1,128)S(1)}, f32[3,1,2,1,128]{4,3,2,1,0:T(1,128)S(1)}, u32[]{:S(2)}, u32[]{:S(2)}) collective-permute-start(f32[3,1,2,1,128]{4,3,2,1,0:T(1,128)S(1)} %get-tuple-element.1023), channel_id=1, source_target_pairs={{0,32},{32,64},{64,96},{96,128},{128,160},{160,192},{192,224},{224... | collective-permute-start | bytes 9224 | tf_op jit(solution)/shard_map/ppermute | solution.py:25
  21.0 11.2 %collective-permute-start.4 = (f32[3,1,2,1,128]{4,3,2,1,0:T(1,128)S(1)}, f32[3,1,2,1,128]{4,3,2,1,0:T(1,128)S(1)}, u32[]{:S(2)}, u32[]{:S(2)}) collective-permute-start(f32[3,1,2,1,128]{4,3,2,1,0:T(1,128)S(1)} %get-tuple-element.1024), channel_id=1, source_target_pairs={{32,0},{64,32},{96,64},{128,96},{160,128},{192,160},{224,192},{256... | collective-permute-start | bytes 9224 | tf_op jit(solution)/shard_map/ppermute | solution.py:28
  32.3 1.3 collective-permute-done.4
  33.6 1.9 %collective-permute-start.2 = (f32[3,1,4,8,128]{4,3,2,1,0:T(8,128)S(1)}, f32[3,1,4,8,128]{4,3,2,1,0:T(8,128)S(1)}, u32[]{:S(2)}, u32[]{:S(2)}) collective-permute-start(f32[3,1,4,8,128]{4,3,2,1,0:T(8,128)S(1)} %pad_maximum_fusion.6), channel_id=1, source_target_pairs={{0,1},{1,2},{2,3},{3,4},{4,5},{5,6},{6,7},{7,0},{8,9},{9,10},{10,1... | collective-permute-start | bytes 147464 | tf_op jit(solution)/shard_map/ppermute | solution.py:25
  35.5 5.4 %collective-permute-start.5 = (f32[3,1,4,8,128]{4,3,2,1,0:T(8,128)S(1)}, f32[3,1,4,8,128]{4,3,2,1,0:T(8,128)S(1)}, u32[]{:S(2)}, u32[]{:S(2)}) collective-permute-start(f32[3,1,4,8,128]{4,3,2,1,0:T(8,128)S(1)} %pad_maximum_fusion.6), channel_id=1, source_target_pairs={{1,0},{2,1},{3,2},{4,3},{5,4},{6,5},{7,6},{0,7},{9,8},{10,9},{11,1... | collective-permute-start | bytes 147464 | tf_op jit(solution)/shard_map/ppermute | solution.py:28
  41.0 6.7 %fusion.129 = (f32[2,8,128]{2,1,0:T(8,128)S(1)}, f32[2,8,128]{2,1,0:T(8,128)S(1)}, f32[2,8,128]{2,1,0:T(8,128)S(1)}, f32[2,8,128]{2,1,0:T(8,128)S(1)}, f32[2,8,1...) fusion(f32[2,8,128]{2,1,0:T(8,128)S(1)} %get-tuple-element.1015, ...), kind=kLoop, calls=%fused_computation.372 | loop fusion | flops 31694848 | bytes 221184 | tf_op jit(solution)/shard_map/reduce_sum | solution.py:52
  48.1 11.7 %fusion.143 = (f32[2,8,128]{2,1,0:T(8,128)S(1)}, f32[2,8,128]{2,1,0:T(8,128)S(1)}, f32[2,8,128]{2,1,0:T(8,128)S(1)}, f32[2,8,128]{2,1,0:T(8,128)S(1)}, f32[2,8,1...) fusion(f32[2,8,128]{2,1,0:T(8,128)S(1)} %get-tuple-element.983,, ...), kind=kLoop, calls=%fused_computation.386 | loop fusion | flops 62078976 | bytes 360448 | tf_op jit(solution)/shard_map/reduce_sum | solution.py:52
  60.1 9.1 %fusion.141 = (f32[2,8,128]{2,1,0:T(8,128)S(1)}, f32[2,8,128]{2,1,0:T(8,128)S(1)}, f32[2,8,128]{2,1,0:T(8,128)S(1)}, f32[2,8,128]{2,1,0:T(8,128)S(1)}, f32[2,8,1...) fusion(f32[2,8,128]{2,1,0:T(8,128)S(1)} %get-tuple-element.989,, ...), kind=kLoop, calls=%fused_computation.384 | loop fusion | flops 47935488 | bytes 294912 | tf_op jit(solution)/shard_map/reduce_sum | solution.py:52
  71.3 1.9 %collective-permute-start.6 = (f32[2,1,2,1,128]{4,3,2,1,0:T(1,128)S(1)}, f32[2,1,2,1,128]{4,3,2,1,0:T(1,128)S(1)}, u32[]{:S(2)}, u32[]{:S(2)}) collective-permute-start(f32[2,1,2,1,128]{4,3,2,1,0:T(1,128)S(1)} %slice.2963), channel_id=1, source_target_pairs={{0,32},{32,64},{64,96},{96,128},{128,160},{160,192},{192,224},{224... | collective-permute-start | bytes 6152 | tf_op jit(solution)/shard_map/ppermute | solution.py:25
  73.4 9.7 %collective-permute-done.6 = f32[2,1,2,1,128]{4,3,2,1,0:T(1,128)S(1)} collective-permute-done((f32[2,1,2,1,128]{4,3,2,1,0:T(1,128)S(1)}, f32[2,1,2,1,128]{4,3,2,1,0:T(1,128)S(1)}, u32[]{:S(2)}, u32[]{:S(2)}) %collective-permute-start.6) | collective-permute-done | bytes 2080 | tf_op jit(solution)/shard_map/ppermute | solution.py:25
  83.1 3.9 %collective-permute-start.7 = (f32[2,1,2,1,128]{4,3,2,1,0:T(1,128)S(1)}, f32[2,1,2,1,128]{4,3,2,1,0:T(1,128)S(1)}, u32[]{:S(2)}, u32[]{:S(2)}) collective-permute-start(f32[2,1,2,1,128]{4,3,2,1,0:T(1,128)S(1)} %get-tuple-element.1007), channel_id=1, source_target_pairs={{32,0},{64,32},{96,64},{128,96},{160,128},{192,160},{224,192},{256... | collective-permute-start | bytes 6152 | tf_op jit(solution)/shard_map/ppermute | solution.py:28
  87.1 1.5 collective-permute-done.7
  88.6 1.9 %collective-permute-start.8 = (f32[4,1,2,1,128]{4,3,2,1,0:T(1,128)S(1)}, f32[4,1,2,1,128]{4,3,2,1,0:T(1,128)S(1)}, u32[]{:S(2)}, u32[]{:S(2)}) collective-permute-start(f32[4,1,2,1,128]{4,3,2,1,0:T(1,128)S(1)} %get-tuple-element.1004), channel_id=1, source_target_pairs={{0,32},{32,64},{64,96},{96,128},{128,160},{160,192},{192,224},{224... | collective-permute-start | bytes 12296 | tf_op jit(solution)/shard_map/ppermute | solution.py:25
  90.6 9.9 %collective-permute-start.9 = (f32[4,1,2,1,128]{4,3,2,1,0:T(1,128)S(1)}, f32[4,1,2,1,128]{4,3,2,1,0:T(1,128)S(1)}, u32[]{:S(2)}, u32[]{:S(2)}) collective-permute-start(f32[4,1,2,1,128]{4,3,2,1,0:T(1,128)S(1)} %get-tuple-element.1003), channel_id=1, source_target_pairs={{32,0},{64,32},{96,64},{128,96},{160,128},{192,160},{224,192},{256... | collective-permute-start | bytes 12296 | tf_op jit(solution)/shard_map/ppermute | solution.py:28
  100.5 1.9 %collective-permute-start.11 = (f32[4,1,1,8,128]{4,3,2,1,0:T(8,128)S(1)}, f32[4,1,1,8,128]{4,3,2,1,0:T(8,128)S(1)}, u32[]{:S(2)}, u32[]{:S(2)}) collective-permute-start(f32[4,1,1,8,128]{4,3,2,1,0:T(8,128)S(1)} %get-tuple-element.1006), channel_id=1, source_target_pairs={{8,0},{16,8},{24,16},{0,24},{9,1},{17,9},{25,17},{1,25},{10,2},{18... | collective-permute-start | bytes 49160 | tf_op jit(solution)/shard_map/ppermute | solution.py:28
  102.5 5.1 %collective-permute-start.10 = (f32[4,1,1,8,128]{4,3,2,1,0:T(8,128)S(1)}, f32[4,1,1,8,128]{4,3,2,1,0:T(8,128)S(1)}, u32[]{:S(2)}, u32[]{:S(2)}) collective-permute-start(f32[4,1,1,8,128]{4,3,2,1,0:T(8,128)S(1)} %get-tuple-element.1005), channel_id=1, source_target_pairs={{0,8},{8,16},{16,24},{24,0},{1,9},{9,17},{17,25},{25,1},{2,10},{10... | collective-permute-start | bytes 49160 | tf_op jit(solution)/shard_map/ppermute | solution.py:25
  107.7 1.3 collective-permute-done.10
  109.0 1.9 %collective-permute-start.12 = (f32[4,1,4,8,128]{4,3,2,1,0:T(8,128)S(1)}, f32[4,1,4,8,128]{4,3,2,1,0:T(8,128)S(1)}, u32[]{:S(2)}, u32[]{:S(2)}) collective-permute-start(f32[4,1,4,8,128]{4,3,2,1,0:T(8,128)S(1)} %pad_maximum_fusion), channel_id=1, source_target_pairs={{0,1},{1,2},{2,3},{3,4},{4,5},{5,6},{6,7},{7,0},{8,9},{9,10},{10,1... | collective-permute-start | bytes 196616 | tf_op jit(solution)/shard_map/ppermute | solution.py:25
  110.9 5.6 %collective-permute-start.13 = (f32[4,1,4,8,128]{4,3,2,1,0:T(8,128)S(1)}, f32[4,1,4,8,128]{4,3,2,1,0:T(8,128)S(1)}, u32[]{:S(2)}, u32[]{:S(2)}) collective-permute-start(f32[4,1,4,8,128]{4,3,2,1,0:T(8,128)S(1)} %pad_maximum_fusion), channel_id=1, source_target_pairs={{1,0},{2,1},{3,2},{4,3},{5,4},{6,5},{7,6},{0,7},{9,8},{10,9},{11,1... | collective-permute-start | bytes 196616 | tf_op jit(solution)/shard_map/ppermute | solution.py:28
  116.6 1.7 collective-permute-done.13
  118.3 2.4 %multiply_reduce_fusion.53 = (f32[2,8,128]{2,1,0:T(8,128)S(1)}, f32[2,8,128]{2,1,0:T(8,128)S(1)}, f32[2,8,128]{2,1,0:T(8,128)S(1)}) fusion(f32[2,8,128]{2,1,0:T(8,128)S(1)} %get-tuple-element.995, f32[2,8,128]{2,1,0:T(8,128)S(1)} %get-tuple-element.955, f32[2,8,128]{2,1,0:T(8,128)S(1)} %get-tuple-element.996, f32[2,8,128]{2,1,0:T(8,128)S(1)} %get-tuple-element.953, ...), kind=kLoop, calls=%fused_computation.302 | loop fusion | flops 7333888 | bytes 90112 | tf_op jit(solution)/shard_map/reduce_sum | solution.py:62
  120.7 5.9 %multiply_reduce_fusion.43 = (f32[2,8,128]{2,1,0:T(8,128)S(1)}, f32[2,8,128]{2,1,0:T(8,128)S(1)}, f32[2,8,128]{2,1,0:T(8,128)S(1)}, f32[2,8,128]{2,1,0:T(8,128)S...) fusion(f32[2,8,128]{2,1,0:T(8,128)S(1)} %get-tuple-element.952,, ...), kind=kLoop, calls=%fused_computation.280 | loop fusion | flops 21215232 | bytes 204800 | tf_op jit(solution)/shard_map/reduce_sum | solution.py:62
  126.7 5.8 %multiply_reduce_fusion.40 = (f32[2,8,128]{2,1,0:T(8,128)S(1)}, f32[2,8,128]{2,1,0:T(8,128)S(1)}, f32[2,8,128]{2,1,0:T(8,128)S(1)}, f32[2,8,128]{2,1,0:T(8,128)S...) fusion(f32[2,8,128]{2,1,0:T(8,128)S(1)} %get-tuple-element.949,, ...), kind=kLoop, calls=%fused_computation.270 | loop fusion | flops 21477376 | bytes 204800 | tf_op jit(solution)/shard_map/reduce_sum | solution.py:62
  132.5 7.6 %multiply_reduce_fusion.15 = (f32[2,8,128]{2,1,0:T(8,128)S(1)}, f32[2,8,128]{2,1,0:T(8,128)S(1)}, f32[2,8,128]{2,1,0:T(8,128)S(1)}, f32[2,8,128]{2,1,0:T(8,128)S...) fusion(f32[2,8,128]{2,1,0:T(8,128)S(1)} %get-tuple-element.946,, ...), kind=kLoop, calls=%fused_computation.206 | loop fusion | flops 28811264 | bytes 229376 | tf_op jit(solution)/shard_map/reduce_sum | solution.py:62
  140.1 5.2 %multiply_reduce_fusion.12 = (f32[2,8,128]{2,1,0:T(8,128)S(1)}, f32[2,8,128]{2,1,0:T(8,128)S(1)}, f32[2,8,128]{2,1,0:T(8,128)S(1)}, f32[2,8,128]{2,1,0:T(8,128)S...) fusion(f32[2,8,128]{2,1,0:T(8,128)S(1)} %get-tuple-element.943,, ...), kind=kLoop, calls=%fused_computation.200 | loop fusion | flops 21477376 | bytes 204800 | tf_op jit(solution)/shard_map/reduce_sum | solution.py:62
  145.3 7.4 %multiply_reduce_fusion.9 = (f32[2,8,128]{2,1,0:T(8,128)S(1)}, f32[2,8,128]{2,1,0:T(8,128)S(1)}, f32[2,8,128]{2,1,0:T(8,128)S(1)}, f32[2,8,128]{2,1,0:T(8,128)S(...) fusion(f32[2,8,128]{2,1,0:T(8,128)S(1)} %get-tuple-element.943,, ...), kind=kLoop, calls=%fused_computation.192 | loop fusion | flops 27762688 | bytes 229376 | tf_op jit(solution)/shard_map/reduce_sum | solution.py:62
  152.7 5.2 %multiply_reduce_fusion.7 = (f32[2,8,128]{2,1,0:T(8,128)S(1)}, f32[2,8,128]{2,1,0:T(8,128)S(1)}, f32[2,8,128]{2,1,0:T(8,128)S(1)}, f32[2,8,128]{2,1,0:T(8,128)S(...) fusion(f32[2,8,128]{2,1,0:T(8,128)S(1)} %get-tuple-element.940,, ...), kind=kLoop, calls=%fused_computation.186 | loop fusion | flops 21215232 | bytes 204800 | tf_op jit(solution)/shard_map/reduce_sum | solution.py:62
  157.9 9.6 %multiply_reduce_fusion.2 = (f32[2,8,128]{2,1,0:T(8,128)S(1)}, f32[2,8,128]{2,1,0:T(8,128)S(1)}, f32[2,8,128]{2,1,0:T(8,128)S(1)}, f32[2,8,128]{2,1,0:T(8,128)S(...) fusion(f32[2,8,128]{2,1,0:T(8,128)S(1)} %get-tuple-element.940,, ...), kind=kLoop, calls=%fused_computation.174 | loop fusion | flops 41644032 | bytes 286720 | tf_op jit(solution)/shard_map/reduce_sum | solution.py:62
  167.6 0.2 scatter-add.244
  167.8 0.2 scatter-add.245
  168.0 0.2 scatter-add.249
  168.3 0.2 scatter-add.250
  168.5 0.2 scatter-add.254
  168.7 0.2 scatter-add.255
  168.9 0.2 scatter-add.259
  170.1 0.2 scatter-add.270
  170.5 0.2 scatter-add.275
  170.8 0.2 scatter-add.279
  171.4 1.9 %collective-permute-start.14 = (f32[3,1,2,1,128]{4,3,2,1,0:T(1,128)S(1)}, f32[3,1,2,1,128]{4,3,2,1,0:T(1,128)S(1)}, u32[]{:S(2)}, u32[]{:S(2)}) collective-permute-start(f32[3,1,2,1,128]{4,3,2,1,0:T(1,128)S(1)} %slice.3028), channel_id=1, source_target_pairs={{0,32},{32,64},{64,96},{96,128},{128,160},{160,192},{192,224},{224... | collective-permute-start | bytes 9224 | tf_op jit(solution)/shard_map/ppermute | solution.py:25
  173.5 9.4 %collective-permute-done.14 = f32[3,1,2,1,128]{4,3,2,1,0:T(1,128)S(1)} collective-permute-done((f32[3,1,2,1,128]{4,3,2,1,0:T(1,128)S(1)}, f32[3,1,2,1,128]{4,3,2,1,0:T(1,128)S(1)}, u32[]{:S(2)}, u32[]{:S(2)}) %collective-permute-start.14) | collective-permute-done | bytes 3104 | tf_op jit(solution)/shard_map/ppermute | solution.py:25
  182.9 1.9 %collective-permute-start.15 = (f32[3,1,2,1,128]{4,3,2,1,0:T(1,128)S(1)}, f32[3,1,2,1,128]{4,3,2,1,0:T(1,128)S(1)}, u32[]{:S(2)}, u32[]{:S(2)}) collective-permute-start(f32[3,1,2,1,128]{4,3,2,1,0:T(1,128)S(1)} %get-tuple-element.956), channel_id=1, source_target_pairs={{32,0},{64,32},{96,64},{128,96},{160,128},{192,160},{224,192},{256... | collective-permute-start | bytes 9224 | tf_op jit(solution)/shard_map/ppermute | solution.py:28
  184.9 0.7 fusion.169
  185.6 2.9 %collective-permute-done.15 = f32[3,1,2,1,128]{4,3,2,1,0:T(1,128)S(1)} collective-permute-done((f32[3,1,2,1,128]{4,3,2,1,0:T(1,128)S(1)}, f32[3,1,2,1,128]{4,3,2,1,0:T(1,128)S(1)}, u32[]{:S(2)}, u32[]{:S(2)}) %collective-permute-start.15) | collective-permute-done | bytes 3104 | tf_op jit(solution)/shard_map/ppermute | solution.py:28
  188.5 0.6 broadcast_select_fusion
  (169 shorter events, 4.7 us)
Async XLA Ops:
  0.6 0.7 copy-start
  2.1 31.4 %collective-permute-start.1 = (f32[3,1,1,8,128]{4,3,2,1,0:T(8,128)S(1)}, f32[3,1,1,8,128]{4,3,2,1,0:T(8,128)S(1)}, u32[]{:S(2)}, u32[]{:S(2)}) collective-permute-start(f32[3,1,1,8,128]{4,3,2,1,0:T(8,128)S(1)} %get-tuple-element.1025), channel_id=1, source_target_pairs={{8,0},{16,8},{24,16},{0,24},{9,1},{17,9},{25,17},{1,25},{10,2},{18... | collective-permute-start | bytes 36872 | tf_op jit(solution)/shard_map/ppermute | solution.py:28
  4.9 28.7 %collective-permute-start = (f32[3,1,1,8,128]{4,3,2,1,0:T(8,128)S(1)}, f32[3,1,1,8,128]{4,3,2,1,0:T(8,128)S(1)}, u32[]{:S(2)}, u32[]{:S(2)}) collective-permute-start(f32[3,1,1,8,128]{4,3,2,1,0:T(8,128)S(1)} %get-tuple-element.1026), channel_id=1, source_target_pairs={{0,8},{8,16},{16,24},{24,0},{1,9},{9,17},{17,25},{25,1},{2,10},{10... | collective-permute-start | bytes 36872 | tf_op jit(solution)/shard_map/ppermute | solution.py:25
  19.1 13.2 %collective-permute-start.3 = (f32[3,1,2,1,128]{4,3,2,1,0:T(1,128)S(1)}, f32[3,1,2,1,128]{4,3,2,1,0:T(1,128)S(1)}, u32[]{:S(2)}, u32[]{:S(2)}) collective-permute-start(f32[3,1,2,1,128]{4,3,2,1,0:T(1,128)S(1)} %get-tuple-element.1023), channel_id=1, source_target_pairs={{0,32},{32,64},{64,96},{96,128},{128,160},{160,192},{192,224},{224... | collective-permute-start | bytes 9224 | tf_op jit(solution)/shard_map/ppermute | solution.py:25
  21.0 12.5 %collective-permute-start.4 = (f32[3,1,2,1,128]{4,3,2,1,0:T(1,128)S(1)}, f32[3,1,2,1,128]{4,3,2,1,0:T(1,128)S(1)}, u32[]{:S(2)}, u32[]{:S(2)}) collective-permute-start(f32[3,1,2,1,128]{4,3,2,1,0:T(1,128)S(1)} %get-tuple-element.1024), channel_id=1, source_target_pairs={{32,0},{64,32},{96,64},{128,96},{160,128},{192,160},{224,192},{256... | collective-permute-start | bytes 9224 | tf_op jit(solution)/shard_map/ppermute | solution.py:28
  33.6 7.4 %collective-permute-start.2 = (f32[3,1,4,8,128]{4,3,2,1,0:T(8,128)S(1)}, f32[3,1,4,8,128]{4,3,2,1,0:T(8,128)S(1)}, u32[]{:S(2)}, u32[]{:S(2)}) collective-permute-start(f32[3,1,4,8,128]{4,3,2,1,0:T(8,128)S(1)} %pad_maximum_fusion.6), channel_id=1, source_target_pairs={{0,1},{1,2},{2,3},{3,4},{4,5},{5,6},{6,7},{7,0},{8,9},{9,10},{10,1... | collective-permute-start | bytes 147464 | tf_op jit(solution)/shard_map/ppermute | solution.py:25
  35.5 12.6 %collective-permute-start.5 = (f32[3,1,4,8,128]{4,3,2,1,0:T(8,128)S(1)}, f32[3,1,4,8,128]{4,3,2,1,0:T(8,128)S(1)}, u32[]{:S(2)}, u32[]{:S(2)}) collective-permute-start(f32[3,1,4,8,128]{4,3,2,1,0:T(8,128)S(1)} %pad_maximum_fusion.6), channel_id=1, source_target_pairs={{1,0},{2,1},{3,2},{4,3},{5,4},{6,5},{7,6},{0,7},{9,8},{10,9},{11,1... | collective-permute-start | bytes 147464 | tf_op jit(solution)/shard_map/ppermute | solution.py:28
  71.3 11.8 %collective-permute-start.6 = (f32[2,1,2,1,128]{4,3,2,1,0:T(1,128)S(1)}, f32[2,1,2,1,128]{4,3,2,1,0:T(1,128)S(1)}, u32[]{:S(2)}, u32[]{:S(2)}) collective-permute-start(f32[2,1,2,1,128]{4,3,2,1,0:T(1,128)S(1)} %slice.2963), channel_id=1, source_target_pairs={{0,32},{32,64},{64,96},{96,128},{128,160},{160,192},{192,224},{224... | collective-permute-start | bytes 6152 | tf_op jit(solution)/shard_map/ppermute | solution.py:25
  83.1 5.5 %collective-permute-start.7 = (f32[2,1,2,1,128]{4,3,2,1,0:T(1,128)S(1)}, f32[2,1,2,1,128]{4,3,2,1,0:T(1,128)S(1)}, u32[]{:S(2)}, u32[]{:S(2)}) collective-permute-start(f32[2,1,2,1,128]{4,3,2,1,0:T(1,128)S(1)} %get-tuple-element.1007), channel_id=1, source_target_pairs={{32,0},{64,32},{96,64},{128,96},{160,128},{192,160},{224,192},{256... | collective-permute-start | bytes 6152 | tf_op jit(solution)/shard_map/ppermute | solution.py:28
  88.6 19.0 %collective-permute-start.8 = (f32[4,1,2,1,128]{4,3,2,1,0:T(1,128)S(1)}, f32[4,1,2,1,128]{4,3,2,1,0:T(1,128)S(1)}, u32[]{:S(2)}, u32[]{:S(2)}) collective-permute-start(f32[4,1,2,1,128]{4,3,2,1,0:T(1,128)S(1)} %get-tuple-element.1004), channel_id=1, source_target_pairs={{0,32},{32,64},{64,96},{96,128},{128,160},{160,192},{192,224},{224... | collective-permute-start | bytes 12296 | tf_op jit(solution)/shard_map/ppermute | solution.py:25
  90.6 17.0 %collective-permute-start.9 = (f32[4,1,2,1,128]{4,3,2,1,0:T(1,128)S(1)}, f32[4,1,2,1,128]{4,3,2,1,0:T(1,128)S(1)}, u32[]{:S(2)}, u32[]{:S(2)}) collective-permute-start(f32[4,1,2,1,128]{4,3,2,1,0:T(1,128)S(1)} %get-tuple-element.1003), channel_id=1, source_target_pairs={{32,0},{64,32},{96,64},{128,96},{160,128},{192,160},{224,192},{256... | collective-permute-start | bytes 12296 | tf_op jit(solution)/shard_map/ppermute | solution.py:28
  100.5 7.2 %collective-permute-start.11 = (f32[4,1,1,8,128]{4,3,2,1,0:T(8,128)S(1)}, f32[4,1,1,8,128]{4,3,2,1,0:T(8,128)S(1)}, u32[]{:S(2)}, u32[]{:S(2)}) collective-permute-start(f32[4,1,1,8,128]{4,3,2,1,0:T(8,128)S(1)} %get-tuple-element.1006), channel_id=1, source_target_pairs={{8,0},{16,8},{24,16},{0,24},{9,1},{17,9},{25,17},{1,25},{10,2},{18... | collective-permute-start | bytes 49160 | tf_op jit(solution)/shard_map/ppermute | solution.py:28
  102.5 6.6 %collective-permute-start.10 = (f32[4,1,1,8,128]{4,3,2,1,0:T(8,128)S(1)}, f32[4,1,1,8,128]{4,3,2,1,0:T(8,128)S(1)}, u32[]{:S(2)}, u32[]{:S(2)}) collective-permute-start(f32[4,1,1,8,128]{4,3,2,1,0:T(8,128)S(1)} %get-tuple-element.1005), channel_id=1, source_target_pairs={{0,8},{8,16},{16,24},{24,0},{1,9},{9,17},{17,25},{25,1},{2,10},{10... | collective-permute-start | bytes 49160 | tf_op jit(solution)/shard_map/ppermute | solution.py:25
  109.0 7.6 %collective-permute-start.12 = (f32[4,1,4,8,128]{4,3,2,1,0:T(8,128)S(1)}, f32[4,1,4,8,128]{4,3,2,1,0:T(8,128)S(1)}, u32[]{:S(2)}, u32[]{:S(2)}) collective-permute-start(f32[4,1,4,8,128]{4,3,2,1,0:T(8,128)S(1)} %pad_maximum_fusion), channel_id=1, source_target_pairs={{0,1},{1,2},{2,3},{3,4},{4,5},{5,6},{6,7},{7,0},{8,9},{9,10},{10,1... | collective-permute-start | bytes 196616 | tf_op jit(solution)/shard_map/ppermute | solution.py:25
  110.9 7.3 %collective-permute-start.13 = (f32[4,1,4,8,128]{4,3,2,1,0:T(8,128)S(1)}, f32[4,1,4,8,128]{4,3,2,1,0:T(8,128)S(1)}, u32[]{:S(2)}, u32[]{:S(2)}) collective-permute-start(f32[4,1,4,8,128]{4,3,2,1,0:T(8,128)S(1)} %pad_maximum_fusion), channel_id=1, source_target_pairs={{1,0},{2,1},{3,2},{4,3},{5,4},{6,5},{7,6},{0,7},{9,8},{10,9},{11,1... | collective-permute-start | bytes 196616 | tf_op jit(solution)/shard_map/ppermute | solution.py:28
  171.4 11.5 %collective-permute-start.14 = (f32[3,1,2,1,128]{4,3,2,1,0:T(1,128)S(1)}, f32[3,1,2,1,128]{4,3,2,1,0:T(1,128)S(1)}, u32[]{:S(2)}, u32[]{:S(2)}) collective-permute-start(f32[3,1,2,1,128]{4,3,2,1,0:T(1,128)S(1)} %slice.3028), channel_id=1, source_target_pairs={{0,32},{32,64},{64,96},{96,128},{128,160},{160,192},{192,224},{224... | collective-permute-start | bytes 9224 | tf_op jit(solution)/shard_map/ppermute | solution.py:25
  182.9 5.5 %collective-permute-start.15 = (f32[3,1,2,1,128]{4,3,2,1,0:T(1,128)S(1)}, f32[3,1,2,1,128]{4,3,2,1,0:T(1,128)S(1)}, u32[]{:S(2)}, u32[]{:S(2)}) collective-permute-start(f32[3,1,2,1,128]{4,3,2,1,0:T(1,128)S(1)} %get-tuple-element.956), channel_id=1, source_target_pairs={{32,0},{64,32},{96,64},{128,96},{160,128},{192,160},{224,192},{256... | collective-permute-start | bytes 9224 | tf_op jit(solution)/shard_map/ppermute | solution.py:28
where the time goes:
time: 191 us; the launch traced here: 189 us
  other arithmetic  79.5 us (42%)
  starting transfers between devices  73.5 us (38%)
  waiting for transfers between devices  27.7 us (15%)
  local copies, waits for them, and re-layouts  6.16 us (3%)
  between operations  2.14 us (1%)
    reduce_sum x8, other arithmetic, force_terms(): jnp.sum(factor * delta, -1)  49.1 us
    ppermute x8, starting transfers between devices, with_halo(): lax.ppermute(lax.slice_in_dim(block, 0, width, axis=dim), axis, backward)  42.7 us
    ppermute x8, starting transfers between devices, with_halo(): lax.ppermute(lax.slice_in_dim(block, block.shape[dim] - width, None, axis...  30.8 us
    reduce_sum x3, other arithmetic, density_terms(): jnp.sum(square, -1)  27.5 us
    ppermute x8, waiting for transfers between devices, with_halo(): lax.ppermute(lax.slice_in_dim(block, block.shape[dim] - width, None, axis...  20.4 us
    ppermute x8, waiting for transfers between devices, with_halo(): lax.ppermute(lax.slice_in_dim(block, 0, width, axis=dim), axis, backward)  7.28 us
  transfers between devices with their start and end apart: 16, of which 7 were waited for; matrix products, arithmetic and copies ran while one was open for 4% of the time, Pallas kernels for 0%

commit v1 on v0

v1 whole, which is shorter than its diff:
```python
import jax
import jax.numpy as jnp
from jax import lax
from jax.experimental import pallas as pl
from jax.experimental.pallas import tpu as pltpu
from jax.sharding import PartitionSpec as P

SENTINEL = 4.0
S = 128
NYR = 4
NZR = 10
CELLS = NYR * NZR
SLOTS = NZR + 2
TERMS = 32
KINDS = ((0, 1), (1, 2), (2, 3), (0, 3))
PAIRS = ((1, 2), (0, 3))
USES = ((0, (0,)), (1, (0, 1)), (2, (0,)), (3, (1,)))
F32 = jnp.float32
BF16 = jnp.bfloat16


def split3(value):
    high = value.astype(BF16).astype(F32)
    rest = value - high
    mid = rest.astype(BF16).astype(F32)
    return high, mid, rest - mid


def coordinates(comps, plane):
    rows = lax.broadcasted_iota(jnp.int32, (CELLS, S), 0)
    y_row = (
        (rows >= NZR).astype(jnp.int32)
        + (rows >= 2 * NZR).astype(jnp.int32)
        + (rows >= 3 * NZR).astype(jnp.int32)
    )
    z_row = rows - NZR * y_row
    return (
        comps[0] + (plane - 0.5),
        comps[1] + (y_row.astype(F32) - 2.0),
        comps[2] + (z_row.astype(F32) - 5.0),
    )


def put_terms(t_ref, terms):
    for k, term in enumerate(terms):
        t_ref[k * CELLS : (k + 1) * CELLS, :] = term


def get_terms(t_ref, cell, count):
    return t_ref[pl.ds(cell, count, stride=CELLS), :]


def far_terms(coords):
    one = jnp.ones((CELLS, S), F32)
    zero = jnp.zeros((CELLS, S), F32)
    out = []
    for c in coords:
        h, m, l = split3(c)
        out += [h, h, h, m, m, l]
    norm = coords[0] * coords[0] + coords[1] * coords[1] + coords[2] * coords[2]
    return out + [one, one, one] + list(split3(-4.0 * norm)) + [zero] * 8


def own_terms(coords):
    one = jnp.ones((CELLS, S), F32)
    zero = jnp.zeros((CELLS, S), F32)
    out = []
    for c in coords:
        h, m, l = split3(8.0 * c)
        out += [h, m, l, h, m, h]
    norm = coords[0] * coords[0] + coords[1] * coords[1] + coords[2] * coords[2]
    return out + list(split3(1.0 - 4.0 * norm)) + [one, one, one] + [zero] * 8


def build_far(t_ref, far_ref, plane):
    def step(z, carry):
        for kind, (ya, yb) in enumerate(KINDS):
            both = jnp.concatenate(
                [get_terms(t_ref, ya * NZR + z, TERMS), get_terms(t_ref, yb * NZR + z, TERMS)], 0
            )
            at = pl.multiple_of((z + 1) * S, S)
            far_ref[plane, kind, pl.ds(at, S), :] = both.T.astype(BF16)
        return carry

    lax.fori_loop(0, NZR, step, 0)


def build_own(t_ref, own_ref):
    zero = jnp.zeros((TERMS, S), F32)

    def step(z, carry):
        for pair, (ya, yb) in enumerate(PAIRS):
            a = get_terms(t_ref, ya * NZR + z, TERMS)
            b = get_terms(t_ref, yb * NZR + z, TERMS)
            block = jnp.concatenate(
                [jnp.concatenate([a, zero], 1), jnp.concatenate([zero, b], 1)], 0
            )
            at = pl.multiple_of((z + 1) * 2 * TERMS, 2 * TERMS)
            own_ref[pair, pl.ds(at, 2 * TERMS), :] = block.astype(BF16)
        return carry

    lax.fori_loop(0, NZR, step, 0)


def fold(value):
    return jnp.sum(value.reshape(S // 8, 8, value.shape[-1]), axis=0)


def far_rows(far_ref, plane, kind, slot):
    return far_ref[plane, kind, pl.ds(pl.multiple_of(slot * S, S), S), :]


def own_block(own_ref, pair, slot):
    return own_ref[pair, pl.ds(pl.multiple_of(slot * 2 * TERMS, 2 * TERMS), 2 * TERMS), :]


def closeness(rows, block):
    return jnp.maximum(jnp.dot(rows, block, preferred_element_type=F32), 0.0)


def plane_kernel(pos_ref, far_ref, own_ref, rho_ref, quart_ref, t_ref):
    coords = coordinates([pos_ref[c] for c in range(3)], 0.0)
    for kind in range(4):
        for slot in (0, SLOTS - 1):
            far_ref[0, kind, slot * S : (slot + 1) * S, :] = jnp.zeros((S, 2 * TERMS), BF16)
    for pair in range(2):
        for slot in (0, SLOTS - 1):
            own_ref[pair, slot * 2 * TERMS : (slot + 1) * 2 * TERMS, :] = jnp.zeros(
                (2 * TERMS, 2 * S), BF16
            )
    put_terms(t_ref, far_terms(coords))
    build_far(t_ref, far_ref, 0)
    put_terms(t_ref, own_terms(coords))
    build_own(t_ref, own_ref)
    row = lax.broadcasted_iota(jnp.int32, (S, 2 * S), 0)
    lane = lax.broadcasted_iota(jnp.int32, (S, 2 * S), 1)
    itself = (row == lane) | (row + S == lane)

    def step(z, carry):
        for pair, (ya, yb) in enumerate(PAIRS):
            block = own_block(own_ref, pair, z + 1)
            rho = jnp.zeros((8, 2 * S), F32)
            quart = jnp.zeros((8, 2 * S), F32)
            for kind, pairs in USES:
                if pair not in pairs:
                    continue
                for dz in (-1, 0, 1):
                    weight = closeness(far_rows(far_ref, 0, kind, z + 1 + dz), block)
                    square = weight * weight
                    if dz == 0 and KINDS[kind] == (ya, yb):
                        square = jnp.where(itself, 0.0, square)
                    rho = rho + fold(square)
                    if pair == 0:
                        quart = quart + fold(square * square)
            rho = jnp.sum(rho, 0, keepdims=True)
            rho_ref[pl.ds(ya * NZR + z, 1), :] = rho[:, :S]
            rho_ref[pl.ds(yb * NZR + z, 1), :] = rho[:, S:]
            if pair == 0:
                quart = jnp.sum(quart, 0, keepdims=True)
                quart_ref[pl.ds(z, 1), :] = quart[:, :S]
                quart_ref[pl.ds(NZR + z, 1), :] = quart[:, S:]
        return carry

    lax.fori_loop(0, NZR, step, 0)


def column(row):
    return jnp.broadcast_to(row, (S, S)).T


def force_kernel(
    pos_ref,
    low_ref,
    high_ref,
    far0_ref,
    own_ref,
    rho_ref,
    quart_ref,
    energy_ref,
    forces_ref,
    t_ref,
    far_ref,
    xyz_ref,
    rho_sum_ref,
    quart_sum_ref,
    embed_ref,
    row_ref,
):
    sides = (low_ref, high_ref)
    for p in range(2):
        coords = coordinates([sides[p][c] for c in range(3)], (-1.0, 1.0)[p])
        put_terms(t_ref, far_terms(coords))
        build_far(t_ref, far_ref, p)

    planes = (low_ref, pos_ref, high_ref)
    for plane in range(3):
        local = [planes[plane][c] - 0.5 for c in range(3)]
        high = [v.astype(BF16).astype(F32) for v in local]
        rest = [v - h for v, h in zip(local, high)]
        put_terms(
            t_ref, high + [jnp.ones((CELLS, S), F32)] + rest + [jnp.zeros((CELLS, S), F32)]
        )

        def gather(z, carry, plane=plane):
            for kind, (ya, yb) in enumerate(KINDS[:3]):
                both = jnp.concatenate(
                    [get_terms(t_ref, ya * NZR + z, 8), get_terms(t_ref, yb * NZR + z, 8)], 0
                )
                xyz_ref[plane, kind, pl.ds(pl.multiple_of(z * 16, 16), 16), :] = both.astype(BF16)
            return carry

        lax.fori_loop(0, NZR, gather, 0)

    rho_sum_ref[...] = jnp.zeros(rho_sum_ref.shape, F32)
    quart_sum_ref[...] = jnp.zeros(quart_sum_ref.shape, F32)

    def cross(z, carry):
        for p in range(2):
            across = [jnp.zeros((S, S), F32) for _ in range(NYR)]
            for kind, pairs in USES:
                rows = far_rows(far_ref, p, kind, z + 1)
                total = None
                for dz in (-1, 0, 1):
                    for pair in pairs:
                        weight = closeness(rows, own_block(own_ref, pair, z + 1 + dz))
                        square = weight * weight
                        total = square if total is None else total + square
                        at = pl.ds(pl.multiple_of((z + 1 + dz) * 8, 8), 8)
                        rho_sum_ref[pair, at, :] += fold(square)
                        if pair == 0:
                            quart_sum_ref[at, :] += fold(square * square)
                ya, yb = KINDS[kind]
                across[ya] = across[ya] + total[:, :S]
                across[yb] = across[yb] + total[:, S:]
            for y in range(NYR):
                part = column(sides[p][3, pl.ds(y * NZR + z, 1), :])
                rho = jnp.sum(across[y], 1, keepdims=True) + part
                at = pl.multiple_of((y * NZR + z) * S, S)
                embed_ref[2 * p, pl.ds(at, S), :] = 2.5 * lax.rsqrt(rho + 1.0)
        return carry

    lax.fori_loop(0, NZR, cross, 0)

    def finish(z, carry):
        for pair, ys in enumerate(PAIRS):
            at = pl.ds(pl.multiple_of((z + 1) * 8, 8), 8)
            sums = jnp.sum(rho_sum_ref[pair, at, :], 0, keepdims=True)
            for half, y in enumerate(ys):
                rho = rho_ref[pl.ds(y * NZR + z, 1), :] + sums[:, half * S : (half + 1) * S]
                slope = 2.5 * lax.rsqrt(rho + 1.0)
                row_ref[pl.ds(y * NZR + z, 1), :] = slope
                cell_at = pl.multiple_of((y * NZR + z) * S, S)
                embed_ref[1, pl.ds(cell_at, S), :] = column(slope)
        return carry

    lax.fori_loop(0, NZR, finish, 0)

    def push(i, carry):
        z = i + 1
        rho_at = pl.ds(pl.multiple_of((z + 1) * 8, 8), 8)
        rho_both = jnp.sum(rho_sum_ref[0, rho_at, :], 0, keepdims=True)
        quart_both = jnp.sum(quart_sum_ref[rho_at, :], 0, keepdims=True)
        block = own_block(own_ref, 0, z + 1)
        own = 1.0 + jnp.concatenate(
            [row_ref[pl.ds(NZR + z, 1), :], row_ref[pl.ds(2 * NZR + z, 1), :]], 1
        )
        names = ("all", "x-", "x+", "y-", "y+", "z-", "z+")
        sums = [{n: jnp.zeros((8, S), F32) for n in names} for _ in range(2)]
        for dx in (-1, 0, 1):
            for dy in (-1, 0, 1):
                kind = dy + 1
                for dz in (-1, 0, 1):
                    if dx == 0:
                        rows = far_rows(far0_ref, 0, kind, z + 1 + dz)
                    else:
                        rows = far_rows(far_ref, (dx + 1) // 2, kind, z + 1 + dz)
                    weight = closeness(rows, block)
                    slopes = jnp.concatenate(
                        [
                            embed_ref[
                                dx + 1, pl.ds(pl.multiple_of((y * NZR + z + dz) * S, S), S), :
                            ]
                            for y in KINDS[kind]
                        ],
                        1,
                    )
                    factor = weight * ((own + slopes) - weight * weight)
                    top = factor.astype(BF16)
                    low = (factor - top.astype(F32)).astype(BF16)
                    xyz = xyz_ref[dx + 1, kind, pl.ds(pl.multiple_of((z + dz) * 16, 16), 16), :]
                    both = jnp.dot(xyz, top, preferred_element_type=F32) + jnp.dot(
                        xyz, low, preferred_element_type=F32
                    )
                    keys = ["all"]
                    keys += [axis + "-0+"[d + 1] for axis, d in zip("xyz", (dx, dy, dz)) if d]
                    for half in range(2):
                        part = both[half * 8 : half * 8 + 8, half * S : half * S + S]
                        for key in keys:
                            sums[half][key] = sums[half][key] + part
        for half in range(2):
            y = half + 1
            at = pl.ds(y * NZR + z, 1)
            occupied = pos_ref[0, at, :] < 2.0
            acc = sums[half]
            weight_sum = acc["all"][3:4]
            for c, axis in enumerate("xyz"):
                moved = acc[axis + "+"][3:4] - acc[axis + "-"][3:4]
                centre = acc["all"][c : c + 1] + acc["all"][c + 4 : c + 5]
                force = (centre + moved) - (pos_ref[c, at, :] - 0.5) * weight_sum
                forces_ref[pl.ds((c * 2 + half) * 8 + i, 1), :] = jnp.where(
                    occupied, 0.64 * force, 0.0
                )
            rho = rho_ref[at, :] + rho_both[:, half * S : (half + 1) * S]
            quart = quart_ref[pl.ds(half * NZR + z, 1), :] + quart_both[:, half * S : (half + 1) * S]
            energy = -0.2 * jnp.sqrt(rho + 1.0) + 0.01 * (quart - 2.0 * rho)
            energy_ref[pl.ds(half * 8 + i, 1), :] = jnp.where(occupied, energy, 0.0)
        return carry

    lax.fori_loop(0, NZR - 2, push, 0)


def ring(axis, step):
    count = lax.axis_size(axis)
    return [(i, (i + step) % count) for i in range(count)]


def widen(block, axis, dim):
    low = lax.ppermute(
        lax.slice_in_dim(block, block.shape[dim] - 1, None, axis=dim), axis, ring(axis, 1)
    )
    high = lax.ppermute(lax.slice_in_dim(block, 0, 1, axis=dim), axis, ring(axis, -1))
    return jnp.concatenate([low, block, high], axis=dim)


def plane_sums(plane):
    return pl.pallas_call(
        plane_kernel,
        out_shape=(
            jax.ShapeDtypeStruct((1, 4, SLOTS * S, 2 * TERMS), BF16),
            jax.ShapeDtypeStruct((2, SLOTS * 2 * TERMS, 2 * S), BF16),
            jax.ShapeDtypeStruct((CELLS, S), F32),
            jax.ShapeDtypeStruct((2 * NZR, S), F32),
        ),
        scratch_shapes=[pltpu.VMEM((TERMS * CELLS, S), F32)],
        name="plane",
    )(plane)


def finish_forces(*operands):
    return pl.pallas_call(
        force_kernel,
        out_shape=(
            jax.ShapeDtypeStruct((2 * 8, S), F32),
            jax.ShapeDtypeStruct((3 * 2 * 8, S), F32),
        ),
        scratch_shapes=[
            pltpu.VMEM((TERMS * CELLS, S), F32),
            pltpu.VMEM((2, 4, SLOTS * S, 2 * TERMS), BF16),
            pltpu.VMEM((3, 3, NZR * 16, S), BF16),
            pltpu.VMEM((2, SLOTS * 8, 2 * S), F32),
            pltpu.VMEM((SLOTS * 8, 2 * S), F32),
            pltpu.VMEM((3, CELLS * S, S), F32),
            pltpu.VMEM((CELLS, S), F32),
        ],
        name="forces",
    )(*operands)


def per_device(positions, counts):
    occupied = jnp.arange(S, dtype=jnp.int32) < counts[..., None]
    seated = jnp.where(occupied[None], positions, SENTINEL)[:, 0]
    plane = widen(widen(seated, "gz", 2), "gy", 1).reshape(3, CELLS, S)
    far0, own, rho, quart = plane_sums(plane)
    message = jnp.concatenate([plane, rho[None]], 0)
    low = lax.ppermute(message, "gx", ring("gx", 1))
    high = lax.ppermute(message, "gx", ring("gx", -1))
    energy, forces = finish_forces(plane, low, high, far0, own, rho, quart)
    return (energy.reshape(1, 2, 8, S), forces.reshape(3, 1, 2, 8, S))


def solution(mesh):
    placed = (P(None, "gx", "gy", "gz", None), P("gx", "gy", "gz"))
    return jax.shard_map(
        per_device,
        mesh=mesh,
        in_specs=placed,
        out_specs=(P("gx", "gy", "gz", None), P(None, "gx", "gy", "gz", None)),
        check_vma=False,
    )
```

time: 191 us -> 83.6 us (0.44)
  other arithmetic: 79.5 us -> 2.38 us
  starting transfers between devices: 73.5 us -> 33.2 us
  Pallas kernels: 0 us -> 34.2 us
  waiting for transfers between devices: 27.7 us -> 11.3 us
  local copies, waits for them, and re-layouts: 6.16 us -> 1.28 us
    reduce_sum x11 -> x0, other arithmetic: 76.7 us -> none  [the longest x8 49.1 us: force_terms(): jnp.sum(factor * delta, -1)]
    ppermute x16 -> x6, starting transfers between devices: 73.5 us -> 33.2 us  [the longest x2 21.5 us: widen(): lax.ppermute(lax.slice_in_dim(block, 0, 1, axis=dim), axis, ring(axis, -1))]
    pallas_call x0 -> x2, Pallas kernels: none -> 34.2 us  [the longest x1 26.8 us: finish_forces(): pl.pallas_call(force_kernel, out_shape=(jax.ShapeDtypeStruct((2 * 8, S),...]
    ppermute x16 -> x6, waiting for transfers between devices: 27.7 us -> 11.3 us  [the longest x2 6.2 us: widen(): lax.ppermute(lax.slice_in_dim(block, 0, 1, axis=dim), axis, ring(axis, -1))]
    scatter-add x40 -> x0, local copies, waits for them, and re-layouts: 5.4 us -> none  [the longest x18 2.95 us: per_device(): pushes.at[:, :, :, 1 + step_z:1 + step_z + layers]]
    select_n x3 -> x0, other arithmetic: 2.03 us -> none  [the longest x1 0.74 us: per_device(): seated = jnp.where(occupied[None], positions, SENTINEL)]
  transfers between devices with their start and end apart: 16 -> 6, of which waited for: 7 -> 3; matrix products, arithmetic and copies ran while one was open for 4% -> 0% of each run, Pallas kernels for 0% -> 0%
where the time goes in v1:
time: 83.6 us; the launch traced here: 83.1 us
  Pallas kernels  34.2 us (41%)
  starting transfers between devices  33.2 us (40%)
  waiting for transfers between devices  11.3 us (14%)
  other arithmetic  2.38 us (3%)
  local copies, waits for them, and re-layouts  1.28 us (2%)
    pallas_call x1, Pallas kernels, finish_forces(): pl.pallas_call(force_kernel, out_shape=(jax.ShapeDtypeStruct((2 * 8, S),...  26.8 us
    ppermute x2, starting transfers between devices, widen(): lax.ppermute(lax.slice_in_dim(block, 0, 1, axis=dim), axis, ring(axis, -1))  21.5 us
    pallas_call x1, Pallas kernels, plane_sums(): pl.pallas_call(plane_kernel, out_shape=(jax.ShapeDtypeStruct((1, 4, SLOTS...  7.49 us
    ppermute x2, starting transfers between devices, widen(): lax.ppermute(lax.slice_in_dim(block, block.shape[dim] - 1, None, axis=dim...  7.33 us
    ppermute x2, waiting for transfers between devices, widen(): lax.ppermute(lax.slice_in_dim(block, 0, 1, axis=dim), axis, ring(axis, -1))  6.2 us
    ppermute x1, waiting for transfers between devices, per_device(): low = lax.ppermute(message, 'gx', ring('gx', 1))  5.12 us
    ppermute x1, starting transfers between devices, per_device(): low = lax.ppermute(message, 'gx', ring('gx', 1))  2.41 us
    ppermute x1, starting transfers between devices, per_device(): high = lax.ppermute(message, 'gx', ring('gx', -1))  1.91 us
  transfers between devices with their start and end apart: 6, of which 3 were waited for; matrix products, arithmetic and copies ran while one was open for 0% of the time, Pallas kernels for 0%

profile of v1, /device:TPU:6, one launch (start us, length us, event | category | flops | bytes accessed | tf_op | source)
XLA Modules:
  0.0 83.1 jit_solution(12483346924837683470)
XLA Ops:
  0.6 0.8 iota_compare_fusion
  1.4 0.7 select_bitcast_fusion
  2.1 3.5 %collective-permute-start = (f32[3,2,1,128]{3,2,1,0:T(1,128)S(1)}, f32[3,2,1,128]{3,2,1,0:T(1,128)S(1)}, u32[]{:S(2)}, u32[]{:S(2)}) collective-permute-start(f32[3,2,1,128]{3,2,1,0:T(1,128)S(1)} %get-tuple-element.20), channel_id=1, source_target_pairs={{0,32},{32,64},{64,96},{96,128},{128,160},{160,192},{192,224},{224... | collective-permute-start | bytes 9224 | tf_op jit(solution)/shard_map/ppermute | solution.py:328
  5.6 19.5 %collective-permute-start.1 = (f32[3,2,1,128]{3,2,1,0:T(1,128)S(1)}, f32[3,2,1,128]{3,2,1,0:T(1,128)S(1)}, u32[]{:S(2)}, u32[]{:S(2)}) collective-permute-start(f32[3,2,1,128]{3,2,1,0:T(1,128)S(1)} %get-tuple-element.21), channel_id=1, source_target_pairs={{0,992},{32,0},{64,32},{96,64},{128,96},{160,128},{192,160},{224,1... | collective-permute-start | bytes 9224 | tf_op jit(solution)/shard_map/ppermute | solution.py:331
  25.2 0.0 collective-permute-done
  25.2 1.3 %collective-permute-done.1 = f32[3,2,1,128]{3,2,1,0:T(1,128)S(1)} collective-permute-done((f32[3,2,1,128]{3,2,1,0:T(1,128)S(1)}, f32[3,2,1,128]{3,2,1,0:T(1,128)S(1)}, u32[]{:S(2)}, u32[]{:S(2)}) %collective-permute-start.1) | collective-permute-done | bytes 3104 | tf_op jit(solution)/shard_map/ppermute | solution.py:331
  26.5 3.8 %collective-permute-start.2 = (f32[3,1,10,128]{3,2,1,0:T(8,128)S(1)}, f32[3,1,10,128]{3,2,1,0:T(8,128)S(1)}, u32[]{:S(2)}, u32[]{:S(2)}) collective-permute-start(f32[3,1,10,128]{3,2,1,0:T(8,128)S(1)} %get-tuple-element.18), channel_id=1, source_target_pairs={{0,8},{8,16},{16,24},{24,0},{1,9},{9,17},{17,25},{25,1},{2,10},{10... | collective-permute-start | bytes 46088 | tf_op jit(solution)/shard_map/ppermute | solution.py:328
  30.4 2.0 %collective-permute-start.3 = (f32[3,1,10,128]{3,2,1,0:T(8,128)S(1)}, f32[3,1,10,128]{3,2,1,0:T(8,128)S(1)}, u32[]{:S(2)}, u32[]{:S(2)}) collective-permute-start(f32[3,1,10,128]{3,2,1,0:T(8,128)S(1)} %get-tuple-element.19), channel_id=1, source_target_pairs={{0,24},{8,0},{16,8},{24,16},{1,25},{9,1},{17,9},{25,17},{2,26},{10... | collective-permute-start | bytes 46088 | tf_op jit(solution)/shard_map/ppermute | solution.py:331
  32.4 0.0 collective-permute-done.2
  32.4 4.9 %collective-permute-done.3 = f32[3,1,10,128]{3,2,1,0:T(8,128)S(1)} collective-permute-done((f32[3,1,10,128]{3,2,1,0:T(8,128)S(1)}, f32[3,1,10,128]{3,2,1,0:T(8,128)S(1)}, u32[]{:S(2)}, u32[]{:S(2)}) %collective-permute-start.3) | collective-permute-done | bytes 15392 | tf_op jit(solution)/shard_map/ppermute | solution.py:331
  37.3 0.6 reshape.23.pos_ref
  37.9 7.5 %plane.1 = (bf16[1,4,1536,64]{3,2,1,0:T(8,128)(2,1)}, bf16[2,768,256]{2,1,0:T(8,128)(2,1)}, f32[40,128]{1,0:T(8,128)}, f32[20,128]{1,0:T(8,128)}) custom-call(f32[3,40,128]{2,1,0:T(8,128)} %reshape.23.pos_ref), custom_call_target="tpu_custom_call" | custom-call | tf_op jit(solution)/shard_map/plane/pallas_call | solution.py:336
  45.4 0.9 %pad_maximum_fusion.1 = f32[4,40,128]{2,1,0:T(8,128)S(1)} fusion(f32[1,40,128]{2,1,0:T(8,128)} %bitcast.8, f32[3,40,128]{2,1,0:T(8,128)} %reshape.23.pos_ref), kind=kLoop, calls=%fused_computation.1 | loop fusion | flops 20480 | bytes 163840 | tf_op jit(solution)/shard_map/concatenate | solution.py:374
  46.3 1.9 %collective-permute-start.5 = (f32[4,40,128]{2,1,0:T(8,128)S(1)}, f32[4,40,128]{2,1,0:T(8,128)S(1)}, u32[]{:S(2)}, u32[]{:S(2)}) collective-permute-start(f32[4,40,128]{2,1,0:T(8,128)S(1)} %pad_maximum_fusion.1), channel_id=1, source_target_pairs={{0,7},{1,0},{2,1},{3,2},{4,3},{5,4},{6,5},{7,6},{8,15},{9,8},{10,9... | collective-permute-start | bytes 245768 | tf_op jit(solution)/shard_map/ppermute | solution.py:376
  48.2 2.4 %collective-permute-start.4 = (f32[4,40,128]{2,1,0:T(8,128)S(1)}, f32[4,40,128]{2,1,0:T(8,128)S(1)}, u32[]{:S(2)}, u32[]{:S(2)}) collective-permute-start(f32[4,40,128]{2,1,0:T(8,128)S(1)} %pad_maximum_fusion.1), channel_id=1, source_target_pairs={{0,1},{1,2},{2,3},{3,4},{4,5},{5,6},{6,7},{7,0},{8,9},{9,10},{10,1... | collective-permute-start | bytes 245768 | tf_op jit(solution)/shard_map/ppermute | solution.py:375
  50.6 0.0 collective-permute-done.5.high_ref
  50.6 0.0 copy-start
  50.6 5.1 %collective-permute-done.4.low_ref = f32[4,40,128]{2,1,0:T(8,128)S(1)} collective-permute-done((f32[4,40,128]{2,1,0:T(8,128)S(1)}, f32[4,40,128]{2,1,0:T(8,128)S(1)}, u32[]{:S(2)}, u32[]{:S(2)}) %collective-permute-start.4) | collective-permute-done | bytes 81952 | tf_op jit(solution)/shard_map/ppermute | solution.py:375
  55.7 0.0 copy-start.1
  55.7 0.0 copy-done
  55.7 0.6 copy-done.1
  56.4 26.8 %forces.1 = (f32[16,128]{1,0:T(8,128)}, f32[48,128]{1,0:T(8,128)}) custom-call(f32[3,40,128]{2,1,0:T(8,128)} %reshape.23.pos_ref, f32[4,40,128]{2,1,0:T(8,128)} %copy-done.1, f32[4,40,128]{2,1,0:T(8,128)} %copy-done, bf16[1,4,1536,64]{3,2,1,0:T(8,128)(2,1)} %get-tuple-element.9.far0_ref, bf16[2,768,256]{2,1,0:T(8,128)(2,1)} %get-tuple-element.10.own_ref, ...), custom_call_target="tpu_custom_call" | custom-call | tf_op jit(solution)/shard_map/forces/pallas_call | solution.py:350
  (4 shorter events, 0.0 us)
Async XLA Ops:
  2.1 23.0 %collective-permute-start = (f32[3,2,1,128]{3,2,1,0:T(1,128)S(1)}, f32[3,2,1,128]{3,2,1,0:T(1,128)S(1)}, u32[]{:S(2)}, u32[]{:S(2)}) collective-permute-start(f32[3,2,1,128]{3,2,1,0:T(1,128)S(1)} %get-tuple-element.20), channel_id=1, source_target_pairs={{0,32},{32,64},{64,96},{96,128},{128,160},{160,192},{192,224},{224... | collective-permute-start | bytes 9224 | tf_op jit(solution)/shard_map/ppermute | solution.py:328
  5.6 20.8 %collective-permute-start.1 = (f32[3,2,1,128]{3,2,1,0:T(1,128)S(1)}, f32[3,2,1,128]{3,2,1,0:T(1,128)S(1)}, u32[]{:S(2)}, u32[]{:S(2)}) collective-permute-start(f32[3,2,1,128]{3,2,1,0:T(1,128)S(1)} %get-tuple-element.21), channel_id=1, source_target_pairs={{0,992},{32,0},{64,32},{96,64},{128,96},{160,128},{192,160},{224,1... | collective-permute-start | bytes 9224 | tf_op jit(solution)/shard_map/ppermute | solution.py:331
  26.5 5.9 %collective-permute-start.2 = (f32[3,1,10,128]{3,2,1,0:T(8,128)S(1)}, f32[3,1,10,128]{3,2,1,0:T(8,128)S(1)}, u32[]{:S(2)}, u32[]{:S(2)}) collective-permute-start(f32[3,1,10,128]{3,2,1,0:T(8,128)S(1)} %get-tuple-element.18), channel_id=1, source_target_pairs={{0,8},{8,16},{16,24},{24,0},{1,9},{9,17},{17,25},{25,1},{2,10},{10... | collective-permute-start | bytes 46088 | tf_op jit(solution)/shard_map/ppermute | solution.py:328
  30.4 6.9 %collective-permute-start.3 = (f32[3,1,10,128]{3,2,1,0:T(8,128)S(1)}, f32[3,1,10,128]{3,2,1,0:T(8,128)S(1)}, u32[]{:S(2)}, u32[]{:S(2)}) collective-permute-start(f32[3,1,10,128]{3,2,1,0:T(8,128)S(1)} %get-tuple-element.19), channel_id=1, source_target_pairs={{0,24},{8,0},{16,8},{24,16},{1,25},{9,1},{17,9},{25,17},{2,26},{10... | collective-permute-start | bytes 46088 | tf_op jit(solution)/shard_map/ppermute | solution.py:331
  46.3 4.3 %collective-permute-start.5 = (f32[4,40,128]{2,1,0:T(8,128)S(1)}, f32[4,40,128]{2,1,0:T(8,128)S(1)}, u32[]{:S(2)}, u32[]{:S(2)}) collective-permute-start(f32[4,40,128]{2,1,0:T(8,128)S(1)} %pad_maximum_fusion.1), channel_id=1, source_target_pairs={{0,7},{1,0},{2,1},{3,2},{4,3},{5,4},{6,5},{7,6},{8,15},{9,8},{10,9... | collective-permute-start | bytes 245768 | tf_op jit(solution)/shard_map/ppermute | solution.py:376
  48.2 7.6 %collective-permute-start.4 = (f32[4,40,128]{2,1,0:T(8,128)S(1)}, f32[4,40,128]{2,1,0:T(8,128)S(1)}, u32[]{:S(2)}, u32[]{:S(2)}) collective-permute-start(f32[4,40,128]{2,1,0:T(8,128)S(1)} %pad_maximum_fusion.1), channel_id=1, source_target_pairs={{0,1},{1,2},{2,3},{3,4},{4,5},{5,6},{6,7},{7,0},{8,9},{9,10},{10,1... | collective-permute-start | bytes 245768 | tf_op jit(solution)/shard_map/ppermute | solution.py:375
  50.6 5.1 %copy-start = (f32[4,40,128]{2,1,0:T(8,128)}, f32[4,40,128]{2,1,0:T(8,128)S(1)}, u32[]{:S(2)}) copy-start(f32[4,40,128]{2,1,0:T(8,128)S(1)} %collective-permute-done.5.high_ref) | copy-start | bytes 245764
  55.7 0.6 copy-start.1

commit v2 on v1

v2 whole, which is shorter than its diff:
```python
import functools

import jax
import jax.numpy as jnp
from jax import lax
from jax.experimental import pallas as pl
from jax.experimental.pallas import tpu as pltpu
from jax.sharding import PartitionSpec as P

SENTINEL = 4.0
S = 128
NYR = 4
NZR = 10
CELLS = NYR * NZR
SLOTS = NZR + 2
TERMS = 32
KINDS = ((0, 1), (1, 2), (2, 3), (0, 3))
PAIRS = ((1, 2), (0, 3))
USES = ((0, (0,)), (1, (0, 1)), (2, (0,)), (3, (1,)))
TIERS = (80, 96, S)
OWN = 16
ROLL = 80
VMEM_LIMIT = 24 * 2**20
F32 = jnp.float32
BF16 = jnp.bfloat16


def split3(value):
    high = value.astype(BF16).astype(F32)
    rest = value - high
    mid = rest.astype(BF16).astype(F32)
    return high, mid, rest - mid


def coordinates(comps, plane):
    rows = lax.broadcasted_iota(jnp.int32, (CELLS, S), 0)
    y_row = (
        (rows >= NZR).astype(jnp.int32)
        + (rows >= 2 * NZR).astype(jnp.int32)
        + (rows >= 3 * NZR).astype(jnp.int32)
    )
    z_row = rows - NZR * y_row
    return (
        comps[0] + (plane - 0.5),
        comps[1] + (y_row.astype(F32) - 2.0),
        comps[2] + (z_row.astype(F32) - 5.0),
    )


def put_terms(t_ref, terms):
    for k, term in enumerate(terms):
        t_ref[k * CELLS : (k + 1) * CELLS, :] = term


def get_terms(t_ref, cell, count):
    return t_ref[pl.ds(cell, count, stride=CELLS), :]


def far_terms(coords):
    one = jnp.ones((CELLS, S), F32)
    zero = jnp.zeros((CELLS, S), F32)
    out = []
    for c in coords:
        h, m, l = split3(c)
        out += [h, h, h, m, m, l]
    norm = coords[0] * coords[0] + coords[1] * coords[1] + coords[2] * coords[2]
    return out + [one, one, one] + list(split3(-4.0 * norm)) + [zero] * 8


def own_terms(coords):
    one = jnp.ones((CELLS, S), F32)
    zero = jnp.zeros((CELLS, S), F32)
    out = []
    for c in coords:
        h, m, l = split3(8.0 * c)
        out += [h, m, l, h, m, h]
    norm = coords[0] * coords[0] + coords[1] * coords[1] + coords[2] * coords[2]
    return out + list(split3(1.0 - 4.0 * norm)) + [one, one, one] + [zero] * 8


def build_far(t_ref, far_refs, kinds, rows=S):
    def step(z, carry):
        for kind, far_ref in zip(kinds, far_refs):
            ya, yb = KINDS[kind]
            both = jnp.concatenate(
                [get_terms(t_ref, ya * NZR + z, TERMS), get_terms(t_ref, yb * NZR + z, TERMS)], 0
            )
            at = pl.multiple_of((z + 1) * S, S)
            far_ref[pl.ds(at, rows), :] = both.T[:rows].astype(BF16)
        return carry

    lax.fori_loop(0, NZR, step, 0)


def build_own(t_ref, own_ref, pair):
    zero = jnp.zeros((TERMS, S), F32)
    ya, yb = PAIRS[pair]

    def step(z, carry):
        a = get_terms(t_ref, ya * NZR + z, TERMS)
        b = get_terms(t_ref, yb * NZR + z, TERMS)
        block = jnp.concatenate([jnp.concatenate([a, zero], 1), jnp.concatenate([zero, b], 1)], 0)
        at = pl.multiple_of((z + 1) * 2 * TERMS, 2 * TERMS)
        own_ref[pl.ds(at, 2 * TERMS), :] = block.astype(BF16)
        return carry

    lax.fori_loop(0, NZR, step, 0)


def empty_ends(ref, size):
    for slot in (0, SLOTS - 1):
        ref[slot * size : (slot + 1) * size, :] = jnp.zeros((size, ref.shape[1]), BF16)


def fold(value):
    return jnp.sum(value.reshape(value.shape[0] // 8, 8, value.shape[-1]), axis=0)


def far_rows(far_ref, slot, rows=S):
    return far_ref[pl.ds(pl.multiple_of(slot * S, S), rows), :]


def own_block(own_ref, slot):
    return own_ref[pl.ds(pl.multiple_of(slot * 2 * TERMS, 2 * TERMS), 2 * TERMS), :]


def closeness(rows, block):
    return jnp.maximum(jnp.dot(rows, block, preferred_element_type=F32), 0.0)


def sort_kernel(pos_ref, counts_ref, own_ref, rank_ref, t_ref):
    lane = lax.broadcasted_iota(jnp.int32, (OWN, S), 1)
    occupied = lane < counts_ref[...]
    comps = [jnp.where(occupied, pos_ref[c], SENTINEL) for c in range(3)]
    low = occupied & (comps[0] < 0.5)
    high = occupied & (comps[0] >= 0.5)
    up_to = lax.broadcasted_iota(jnp.int32, (S, S), 0) <= lax.broadcasted_iota(
        jnp.int32, (S, S), 1
    )
    up_to = jnp.where(up_to, 1.0, 0.0).astype(BF16)
    flags = jnp.concatenate([jnp.where(m, 1.0, 0.0) for m in (low, high, ~occupied)], 0)
    before = jnp.dot(flags.astype(BF16), up_to, preferred_element_type=F32)
    lows, highs, blanks = before[:OWN], before[OWN : 2 * OWN], before[2 * OWN :]
    all_low = jnp.max(lows, axis=1, keepdims=True)
    rank = jnp.where(low, lows - 1.0, jnp.where(high, S - highs, all_low + blanks - 1.0))
    rank_ref[...] = rank
    terms = []
    for c in comps:
        terms += list(split3(c))
    for k, term in enumerate(terms + [jnp.zeros((OWN, S), F32)] * 7):
        t_ref[k * OWN : (k + 1) * OWN, :] = term
    slot = lax.broadcasted_iota(jnp.int32, (S, S), 0).astype(F32)
    for cell in range(OWN):
        chosen = jnp.where(slot == rank[cell : cell + 1], 1.0, 0.0).astype(BF16)
        rows = t_ref[pl.ds(cell, 16, stride=OWN), :].astype(BF16)
        moved = lax.dot_general(
            rows, chosen, (((1,), (1,)), ((), ())), preferred_element_type=F32
        )
        for c in range(3):
            own_ref[c, cell : cell + 1, :] = (
                moved[3 * c : 3 * c + 1] + moved[3 * c + 1 : 3 * c + 2]
            ) + moved[3 * c + 2 : 3 * c + 3]


def row_sums(z, far_refs, kinds, own_ref, pair, rho, quart):
    block = own_block(own_ref, z + 1)
    row = lax.broadcasted_iota(jnp.int32, (S, 2 * S), 0)
    lane = lax.broadcasted_iota(jnp.int32, (S, 2 * S), 1)
    itself = (row == lane) | (row + S == lane)
    for kind, far_ref in zip(kinds, far_refs):
        for dz in (-1, 0, 1):
            weight = closeness(far_rows(far_ref, z + 1 + dz), block)
            square = weight * weight
            if dz == 0 and KINDS[kind] == PAIRS[pair]:
                square = jnp.where(itself, 0.0, square)
            rho = rho + fold(square)
            if pair == 0:
                quart = quart + fold(square * square)
    return jnp.sum(rho, 0, keepdims=True), jnp.sum(quart, 0, keepdims=True)


def pair_row_kernel(pos_ref, far_ref, own_ref, sums_ref, t_ref, whole_ref):
    for c in range(3):
        for y in range(2):
            whole_ref[c, (y + 1) * NZR : (y + 2) * NZR, :] = pos_ref[c, y]
            whole_ref[c, y * 3 * NZR : (y * 3 + 1) * NZR, :] = jnp.zeros((NZR, S), F32)
    coords = coordinates([whole_ref[c] for c in range(3)], 0.0)
    empty_ends(far_ref, S)
    empty_ends(own_ref, 2 * TERMS)
    put_terms(t_ref, far_terms(coords))
    build_far(t_ref, [far_ref], [1])
    put_terms(t_ref, own_terms(coords))
    build_own(t_ref, own_ref, 0)
    zero = jnp.zeros((8, 2 * S), F32)

    def step(z, carry):
        rho, quart = row_sums(z, [far_ref], [1], own_ref, 0, zero, zero)
        sums_ref[pl.ds(z, 1), :] = rho
        sums_ref[pl.ds(NZR + z, 1), :] = quart
        return carry

    lax.fori_loop(0, NZR, step, 0)


def plane_kernel(
    pos_ref,
    below_ref,
    above_ref,
    mid_ref,
    own_ref,
    sums_ref,
    plane_ref,
    far_a_ref,
    far_b_ref,
    own_halo_ref,
    quart_ref,
    t_ref,
    far_c_ref,
):
    for c in range(3):
        plane_ref[c, 0:NZR, :] = below_ref[c, 0]
        plane_ref[c, NZR : 2 * NZR, :] = pos_ref[c, 0]
        plane_ref[c, 2 * NZR : 3 * NZR, :] = pos_ref[c, 1]
        plane_ref[c, 3 * NZR :, :] = above_ref[c, 0]
    coords = coordinates([plane_ref[c] for c in range(3)], 0.0)
    for ref in (far_a_ref, far_b_ref, far_c_ref):
        empty_ends(ref, S)
    empty_ends(own_halo_ref, 2 * TERMS)
    put_terms(t_ref, far_terms(coords))
    build_far(t_ref, [far_a_ref, far_b_ref, far_c_ref], [0, 2, 3])
    put_terms(t_ref, own_terms(coords))
    build_own(t_ref, own_halo_ref, 1)
    zero = jnp.zeros((8, 2 * S), F32)

    def step(z, carry):
        rho, quart = row_sums(z, [far_a_ref, far_b_ref], [0, 2], own_ref, 0, zero, zero)
        rho = rho + sums_ref[pl.ds(z, 1), :]
        quart = quart + sums_ref[pl.ds(NZR + z, 1), :]
        plane_ref[3, pl.ds(NZR + z, 1), :] = rho[:, :S]
        plane_ref[3, pl.ds(2 * NZR + z, 1), :] = rho[:, S:]
        quart_ref[pl.ds(z, 1), :] = quart[:, :S]
        quart_ref[pl.ds(NZR + z, 1), :] = quart[:, S:]
        rho, _ = row_sums(z, [mid_ref, far_c_ref], [1, 3], own_halo_ref, 1, zero, zero)
        plane_ref[3, pl.ds(z, 1), :] = rho[:, :S]
        plane_ref[3, pl.ds(3 * NZR + z, 1), :] = rho[:, S:]
        return carry

    lax.fori_loop(0, NZR, step, 0)


def column(row, rows=S):
    return jnp.broadcast_to(row, (S, S)).T[:rows]


def force_kernel(
    plane_ref,
    low_ref,
    high_ref,
    mid_ref,
    far_a_ref,
    far_b_ref,
    own_ref,
    own_halo_ref,
    quart_ref,
    rank_ref,
    energy_ref,
    forces_ref,
    t_ref,
    rolled_ref,
    far_ref,
    xyz_ref,
    rho_sum_ref,
    quart_sum_ref,
    embed_ref,
    row_ref,
    done_ref,
):
    lane = lax.broadcasted_iota(jnp.int32, (CELLS, S), 1)
    for c in range(4):
        rolled_ref[c] = pltpu.roll(low_ref[c], ROLL, 1)
    x_low, x_high = rolled_ref[0], high_ref[0]
    last = jnp.maximum(
        jnp.where((x_low > 0.5) & (x_low < 2.0), lane, -1),
        jnp.where(x_high < 0.5, lane, -1),
    )
    needed = jnp.max(last) + 1
    own_pairs = (own_ref, own_halo_ref)
    far0 = (far_a_ref, mid_ref, far_b_ref)
    sides = (rolled_ref, high_ref)
    rho_sum_ref[...] = jnp.zeros(rho_sum_ref.shape, F32)
    quart_sum_ref[...] = jnp.zeros(quart_sum_ref.shape, F32)

    planes = (rolled_ref, plane_ref, high_ref)
    for plane in range(3):
        local = [planes[plane][c] - 0.5 for c in range(3)]
        high = [v.astype(BF16).astype(F32) for v in local]
        rest = [v - h for v, h in zip(local, high)]
        put_terms(
            t_ref, high + [jnp.ones((CELLS, S), F32)] + rest + [jnp.zeros((CELLS, S), F32)]
        )

        def gather(z, carry, plane=plane):
            for kind, (ya, yb) in enumerate(KINDS[:3]):
                both = jnp.concatenate(
                    [get_terms(t_ref, ya * NZR + z, 8), get_terms(t_ref, yb * NZR + z, 8)], 0
                )
                xyz_ref[plane, kind, pl.ds(pl.multiple_of(z * 16, 16), 16), :] = both.astype(BF16)
            return carry

        lax.fori_loop(0, NZR, gather, 0)

    def with_rows(count):
        for p in range(2):
            coords = coordinates([sides[p][c] for c in range(3)], (-1.0, 1.0)[p])
            put_terms(t_ref, far_terms(coords))
            build_far(t_ref, [far_ref.at[p, k] for k in range(4)], range(4), count)

        def cross(z, carry):
            for p in range(2):
                across = [None] * NYR
                for kind, pairs in USES:
                    rows = far_rows(far_ref.at[p, kind], z + 1, count)
                    total = None
                    for dz in (-1, 0, 1):
                        for pair in pairs:
                            weight = closeness(rows, own_block(own_pairs[pair], z + 1 + dz))
                            square = weight * weight
                            total = square if total is None else total + square
                            at = pl.ds(pl.multiple_of((z + 1 + dz) * 8, 8), 8)
                            rho_sum_ref[pair, at, :] += fold(square)
                            if pair == 0:
                                quart_sum_ref[at, :] += fold(square * square)
                    for half, y in enumerate(KINDS[kind]):
                        part = total[:, half * S : (half + 1) * S]
                        across[y] = part if across[y] is None else across[y] + part
                for y in range(NYR):
                    part = column(sides[p][3, pl.ds(y * NZR + z, 1), :], count)
                    rho = jnp.sum(across[y], 1, keepdims=True) + part
                    at = pl.multiple_of((y * NZR + z) * S, S)
                    embed_ref[2 * p, pl.ds(at, count), :] = 2.5 * lax.rsqrt(rho + 1.0)
            return carry

        lax.fori_loop(0, NZR, cross, 0)

        def finish(z, carry):
            for pair, ys in enumerate(PAIRS):
                at = pl.ds(pl.multiple_of((z + 1) * 8, 8), 8)
                sums = jnp.sum(rho_sum_ref[pair, at, :], 0, keepdims=True)
                for half, y in enumerate(ys):
                    rho = plane_ref[3, pl.ds(y * NZR + z, 1), :] + sums[:, half * S : half * S + S]
                    slope = 2.5 * lax.rsqrt(rho + 1.0)
                    row_ref[pl.ds(y * NZR + z, 1), :] = slope
                    cell_at = pl.multiple_of((y * NZR + z) * S, S)
                    embed_ref[1, pl.ds(cell_at, S), :] = column(slope)
            return carry

        lax.fori_loop(0, NZR, finish, 0)

        def push(i, carry):
            z = i + 1
            rho_at = pl.ds(pl.multiple_of((z + 1) * 8, 8), 8)
            rho_both = jnp.sum(rho_sum_ref[0, rho_at, :], 0, keepdims=True)
            quart_both = jnp.sum(quart_sum_ref[rho_at, :], 0, keepdims=True)
            block = own_block(own_ref, z + 1)
            own = 1.0 + jnp.concatenate(
                [row_ref[pl.ds(NZR + z, 1), :], row_ref[pl.ds(2 * NZR + z, 1), :]], 1
            )
            names = ("all", "x-", "x+", "y-", "y+", "z-", "z+")
            sums = [{n: jnp.zeros((8, S), F32) for n in names} for _ in range(2)]
            for dx in (-1, 0, 1):
                used = S if dx == 0 else count
                for dy in (-1, 0, 1):
                    kind = dy + 1
                    for dz in (-1, 0, 1):
                        if dx == 0:
                            rows = far_rows(far0[kind], z + 1 + dz)
                        else:
                            rows = far_rows(far_ref.at[(dx + 1) // 2, kind], z + 1 + dz, count)
                        weight = closeness(rows, block)
                        slopes = jnp.concatenate(
                            [
                                embed_ref[
                                    dx + 1,
                                    pl.ds(pl.multiple_of((y * NZR + z + dz) * S, S), used),
                                    :,
                                ]
                                for y in KINDS[kind]
                            ],
                            1,
                        )
                        factor = weight * ((own + slopes) - weight * weight)
                        top = factor.astype(BF16)
                        low = (factor - top.astype(F32)).astype(BF16)
                        xyz = xyz_ref[
                            dx + 1, kind, pl.ds(pl.multiple_of((z + dz) * 16, 16), 16), :
                        ][:, :used]
                        both = jnp.dot(xyz, top, preferred_element_type=F32) + jnp.dot(
                            xyz, low, preferred_element_type=F32
                        )
                        keys = ["all"]
                        keys += [a + "-0+"[d + 1] for a, d in zip("xyz", (dx, dy, dz)) if d]
                        for half in range(2):
                            part = both[half * 8 : half * 8 + 8, half * S : half * S + S]
                            for key in keys:
                                sums[half][key] = sums[half][key] + part
            for half in range(2):
                y = half + 1
                at = pl.ds(y * NZR + z, 1)
                occupied = plane_ref[0, at, :] < 2.0
                acc = sums[half]
                weight_sum = acc["all"][3:4]
                rho = plane_ref[3, at, :] + rho_both[:, half * S : (half + 1) * S]
                quart = (
                    quart_ref[pl.ds(half * NZR + z, 1), :]
                    + quart_both[:, half * S : (half + 1) * S]
                )
                results = [-0.2 * jnp.sqrt(rho + 1.0) + 0.01 * (quart - 2.0 * rho)]
                for c, axis in enumerate("xyz"):
                    moved = acc[axis + "+"][3:4] - acc[axis + "-"][3:4]
                    centre = acc["all"][c : c + 1] + acc["all"][c + 4 : c + 5]
                    force = (centre + moved) - (plane_ref[c, at, :] - 0.5) * weight_sum
                    results.append(0.64 * force)
                for k, result in enumerate(results):
                    done_ref[pl.ds(k * OWN + half * 8 + i, 1), :] = jnp.where(
                        occupied, result, 0.0
                    )
            return carry

        lax.fori_loop(0, NZR - 2, push, 0)

    floor = 0
    for count in TIERS:
        pl.when((needed > floor if floor else needed >= 0) & (needed <= count))(
            functools.partial(with_rows, count)
        )
        floor = count

    for k, part in enumerate(split3(done_ref[...])):
        t_ref[k * 4 * OWN : (k + 1) * 4 * OWN, :] = part
    slot = lax.broadcasted_iota(jnp.int32, (S, S), 0).astype(F32)
    for cell in range(OWN):
        chosen = jnp.where(slot == rank_ref[cell : cell + 1, :], 1.0, 0.0).astype(BF16)
        rows = t_ref[pl.ds(cell, 16, stride=OWN), :].astype(BF16)
        moved = jnp.dot(rows, chosen, preferred_element_type=F32)
        moved = (moved[0:4] + moved[4:8]) + moved[8:12]
        energy_ref[cell : cell + 1, :] = moved[0:1]
        for c in range(3):
            forces_ref[c * OWN + cell : c * OWN + cell + 1, :] = moved[c + 1 : c + 2]


def ring(axis, step):
    count = lax.axis_size(axis)
    return [(i, (i + step) % count) for i in range(count)]


def kernel_call(body, outs, scratch, name):
    return pl.pallas_call(
        body,
        out_shape=tuple(jax.ShapeDtypeStruct(shape, dtype) for shape, dtype in outs),
        scratch_shapes=[pltpu.VMEM(shape, dtype) for shape, dtype in scratch],
        compiler_params=pltpu.CompilerParams(vmem_limit_bytes=VMEM_LIMIT),
        name=name,
    )


FAR = ((SLOTS * S, 2 * TERMS), BF16)
OWN_BLOCKS = ((SLOTS * 2 * TERMS, 2 * S), BF16)
TERM_ROWS = ((TERMS * CELLS, S), F32)


def sort_cells(positions, counts):
    return kernel_call(
        sort_kernel, [((3, OWN, S), F32), ((OWN, S), F32)], [((16 * OWN, S), F32)], "sort"
    )(positions, counts)


def pair_row(rows):
    return kernel_call(
        pair_row_kernel,
        [FAR, OWN_BLOCKS, ((2 * NZR, 2 * S), F32)],
        [TERM_ROWS, ((3, CELLS, S), F32)],
        "rows",
    )(rows)


def plane_sums(rows, below, above, mid, own, sums):
    return kernel_call(
        plane_kernel,
        [((4, CELLS, S), F32), FAR, FAR, OWN_BLOCKS, ((2 * NZR, S), F32)],
        [TERM_ROWS, FAR],
        "plane",
    )(rows, below, above, mid, own, sums)


def finish_forces(*operands):
    return kernel_call(
        force_kernel,
        [((OWN, S), F32), ((3 * OWN, S), F32)],
        [
            TERM_ROWS,
            ((4, CELLS, S), F32),
            ((2, 4, SLOTS * S, 2 * TERMS), BF16),
            ((3, 3, NZR * 16, S), BF16),
            ((2, SLOTS * 8, 2 * S), F32),
            ((SLOTS * 8, 2 * S), F32),
            ((3, CELLS * S, S), F32),
            ((CELLS, S), F32),
            ((4 * OWN, S), F32),
        ],
        "forces",
    )(*operands)


def per_device(positions, counts):
    sorted_own, rank = sort_cells(positions.reshape(3, OWN, S), counts.reshape(OWN, 1))
    cells = sorted_own.reshape(3, 2, 8, S)
    behind = lax.ppermute(cells[:, :, 7:8], "gz", ring("gz", 1))
    ahead = lax.ppermute(cells[:, :, 0:1], "gz", ring("gz", -1))
    rows = jnp.concatenate([behind, cells, ahead], axis=2)
    below = lax.ppermute(rows[:, 1:2], "gy", ring("gy", 1))
    above = lax.ppermute(rows[:, 0:1], "gy", ring("gy", -1))
    mid, own, sums = pair_row(rows)
    plane, far_a, far_b, own_halo, quart = plane_sums(rows, below, above, mid, own, sums)
    low = lax.ppermute(plane, "gx", ring("gx", 1))
    high = lax.ppermute(plane, "gx", ring("gx", -1))
    energy, forces = finish_forces(
        plane, low, high, mid, far_a, far_b, own, own_halo, quart, rank
    )
    return (energy.reshape(1, 2, 8, S), forces.reshape(3, 1, 2, 8, S))


def solution(mesh):
    placed = (P(None, "gx", "gy", "gz", None), P("gx", "gy", "gz"))
    return jax.shard_map(
        per_device,
        mesh=mesh,
        in_specs=placed,
        out_specs=(P("gx", "gy", "gz", None), P(None, "gx", "gy", "gz", None)),
        check_vma=False,
    )
```

time: 83.6 us -> 76.7 us (0.917)
  waiting for transfers between devices: 11.3 us -> 6.92 us
  Pallas kernels: 34.2 us -> 31.3 us
  other arithmetic: 2.38 us -> 0.01 us
  starting transfers between devices: 33.2 us -> 35.2 us
    ppermute x6, waiting for transfers between devices: 11.3 us -> 6.92 us  [the longest x1 5.52 us: per_device(): low = lax.ppermute(plane, 'gx', ring('gx', 1))]
    pallas_call x2 -> x4, Pallas kernels: 34.2 us -> 31.3 us  [the longest x1 22.1 us: finish_forces(): kernel_call(force_kernel, [((OWN, S), F32), ((3 * OWN, S), F32)], [TERM_R...]
    ppermute x6, starting transfers between devices: 33.2 us -> 35.2 us  [the longest x1 19.5 us: per_device(): ahead = lax.ppermute(cells[:, :, 0:1], 'gz', ring('gz', -1))]
    concatenate x3 -> x1, other arithmetic: 0.88 us -> 0.01 us  [per_device(): rows = jnp.concatenate([behind, cells, ahead], axis=2)]
  transfers between devices with their start and end apart: 6 -> 6, of which waited for: 3 -> 3; matrix products, arithmetic and copies ran while one was open for 0% -> 0% of each run, Pallas kernels for 0% -> 5%
where the time goes in v2:
time: 76.7 us; the launch traced here: 75.7 us
  starting transfers between devices  35.2 us (46%)
  Pallas kernels  31.3 us (41%)
  waiting for transfers between devices  6.92 us (9%)
  local copies, waits for them, and re-layouts  1.52 us (2%)
    pallas_call x1, Pallas kernels, finish_forces(): kernel_call(force_kernel, [((OWN, S), F32), ((3 * OWN, S), F32)], [TERM_R...  22.1 us
    ppermute x1, starting transfers between devices, per_device(): ahead = lax.ppermute(cells[:, :, 0:1], 'gz', ring('gz', -1))  19.5 us
    ppermute x1, waiting for transfers between devices, per_device(): low = lax.ppermute(plane, 'gx', ring('gx', 1))  5.52 us
    pallas_call x1, Pallas kernels, plane_sums(): kernel_call(plane_kernel, [((4, CELLS, S), F32), FAR, FAR, OWN_BLOCKS, ((...  5.02 us
    ppermute x1, starting transfers between devices, per_device(): below = lax.ppermute(rows[:, 1:2], 'gy', ring('gy', 1))  4.32 us
    pallas_call x1, Pallas kernels, pair_row(): kernel_call(pair_row_kernel, [FAR, OWN_BLOCKS, ((2 * NZR, 2 * S), F32)],...  3.49 us
    ppermute x1, starting transfers between devices, per_device(): behind = lax.ppermute(cells[:, :, 7:8], 'gz', ring('gz', 1))  3.48 us
    ppermute x1, starting transfers between devices, per_device(): high = lax.ppermute(plane, 'gx', ring('gx', -1))  3.22 us
  transfers between devices with their start and end apart: 6, of which 3 were waited for; matrix products, arithmetic and copies ran while one was open for 0% of the time, Pallas kernels for 5%

profile of v2, /device:TPU:6, one launch (start us, length us, event | category | flops | bytes accessed | tf_op | source)
XLA Modules:
  0.0 75.7 jit_solution(17046373492508864586)
XLA Ops:
  0.6 0.8 reshape.24.counts_ref
  1.4 0.0 copy-start
  1.4 0.7 copy-done
  2.1 0.6 sort.1
  2.8 3.5 %collective-permute-start = (f32[3,2,1,128]{3,2,1,0:T(1,128)S(1)}, f32[3,2,1,128]{3,2,1,0:T(1,128)S(1)}, u32[]{:S(2)}, u32[]{:S(2)}) collective-permute-start(f32[3,2,1,128]{3,2,1,0:T(1,128)S(1)} %get-tuple-element.30), channel_id=1, source_target_pairs={{0,32},{32,64},{64,96},{96,128},{128,160},{160,192},{192,224},{224... | collective-permute-start | bytes 9224 | tf_op jit(solution)/shard_map/ppermute | solution.py:517
  6.3 19.5 %collective-permute-start.1 = (f32[3,2,1,128]{3,2,1,0:T(1,128)S(1)}, f32[3,2,1,128]{3,2,1,0:T(1,128)S(1)}, u32[]{:S(2)}, u32[]{:S(2)}) collective-permute-start(f32[3,2,1,128]{3,2,1,0:T(1,128)S(1)} %get-tuple-element.31), channel_id=1, source_target_pairs={{0,992},{32,0},{64,32},{96,64},{128,96},{160,128},{192,160},{224,1... | collective-permute-start | bytes 9224 | tf_op jit(solution)/shard_map/ppermute | solution.py:518
  25.8 0.0 collective-permute-done
  25.8 1.3 %collective-permute-done.1 = f32[3,2,1,128]{3,2,1,0:T(1,128)S(1)} collective-permute-done((f32[3,2,1,128]{3,2,1,0:T(1,128)S(1)}, f32[3,2,1,128]{3,2,1,0:T(1,128)S(1)}, u32[]{:S(2)}, u32[]{:S(2)}) %collective-permute-start.1) | collective-permute-done | bytes 3104 | tf_op jit(solution)/shard_map/ppermute | solution.py:518
  27.2 2.7 %collective-permute-start.3 = (f32[3,1,10,128]{3,2,1,0:T(8,128)S(1)}, f32[3,1,10,128]{3,2,1,0:T(8,128)S(1)}, u32[]{:S(2)}, u32[]{:S(2)}) collective-permute-start(f32[3,1,10,128]{3,2,1,0:T(8,128)S(1)} %get-tuple-element.28), channel_id=1, source_target_pairs={{0,24},{8,0},{16,8},{24,16},{1,25},{9,1},{17,9},{25,17},{2,26},{10... | collective-permute-start | bytes 46088 | tf_op jit(solution)/shard_map/ppermute | solution.py:521
  29.9 4.3 %collective-permute-start.2 = (f32[3,1,10,128]{3,2,1,0:T(8,128)S(1)}, f32[3,1,10,128]{3,2,1,0:T(8,128)S(1)}, u32[]{:S(2)}, u32[]{:S(2)}) collective-permute-start(f32[3,1,10,128]{3,2,1,0:T(8,128)S(1)} %get-tuple-element.29), channel_id=1, source_target_pairs={{0,8},{8,16},{16,24},{24,0},{1,9},{9,17},{17,25},{25,1},{2,10},{10... | collective-permute-start | bytes 46088 | tf_op jit(solution)/shard_map/ppermute | solution.py:520
  34.2 3.5 %rows.1 = (bf16[1536,64]{1,0:T(8,128)(2,1)S(1)}, bf16[768,256]{1,0:T(8,128)(2,1)S(1)}, f32[20,256]{1,0:T(8,128)S(1)}) custom-call(f32[3,2,10,128]{3,2,1,0:T(8,128)S(1)} %pad_maximum_fusion.pos_ref), custom_call_target="tpu_custom_call" | custom-call | tf_op jit(solution)/shard_map/rows/pallas_call | solution.py:478
  37.7 0.0 collective-permute-done.3.above_ref
  37.7 0.0 collective-permute-done.2.below_ref
  37.7 5.0 %plane.1 = (f32[4,40,128]{2,1,0:T(8,128)S(1)}, bf16[1536,64]{1,0:T(8,128)(2,1)S(1)}, bf16[1536,64]{1,0:T(8,128)(2,1)S(1)}, bf16[768,256]{1,0:T(8,128)(2,1)S(1)}, f32[20,128]{1,0:T(8,128)S(1)}) custom-call(f32[3,2,10,128]{3,2,1,0:T(8,128)S(1)} %pad_maximum_fusion.pos_ref, f32[3,1,10,128]{3,2,1,0:T(8,128)S(1)} %collective-permute-done.2.below_ref, ...), custom_call_target="tpu_custom_call" | custom-call | tf_op jit(solution)/shard_map/plane/pallas_call | solution.py:487
  42.8 3.2 %collective-permute-start.5 = (f32[4,40,128]{2,1,0:T(8,128)S(1)}, f32[4,40,128]{2,1,0:T(8,128)S(1)}, u32[]{:S(2)}, u32[]{:S(2)}) collective-permute-start(f32[4,40,128]{2,1,0:T(8,128)S(1)} %get-tuple-element.18.plane_ref), channel_id=1, source_target_pairs={{0,7},{1,0},{2,1},{3,2},{4,3},{5,4},{6,5},{7,6},{8,15},{9,8},{10,9... | collective-permute-start | bytes 245768 | tf_op jit(solution)/shard_map/ppermute | solution.py:525
  46.0 1.9 %collective-permute-start.4 = (f32[4,40,128]{2,1,0:T(8,128)S(1)}, f32[4,40,128]{2,1,0:T(8,128)S(1)}, u32[]{:S(2)}, u32[]{:S(2)}) collective-permute-start(f32[4,40,128]{2,1,0:T(8,128)S(1)} %get-tuple-element.18.plane_ref), channel_id=1, source_target_pairs={{0,1},{1,2},{2,3},{3,4},{4,5},{5,6},{6,7},{7,0},{8,9},{9,10},{10,1... | collective-permute-start | bytes 245768 | tf_op jit(solution)/shard_map/ppermute | solution.py:524
  47.9 0.1 collective-permute-done.5.high_ref
  48.0 5.5 %collective-permute-done.4.low_ref = f32[4,40,128]{2,1,0:T(8,128)S(1)} collective-permute-done((f32[4,40,128]{2,1,0:T(8,128)S(1)}, f32[4,40,128]{2,1,0:T(8,128)S(1)}, u32[]{:S(2)}, u32[]{:S(2)}) %collective-permute-start.4) | collective-permute-done | bytes 81952 | tf_op jit(solution)/shard_map/ppermute | solution.py:524
  53.6 22.1 %forces.1 = (f32[16,128]{1,0:T(8,128)}, f32[48,128]{1,0:T(8,128)}) custom-call(f32[4,40,128]{2,1,0:T(8,128)S(1)} %get-tuple-element.18.plane_ref, f32[4,40,128]{2,1,0:T(8,128)S(1)} %collective-permute-done.4.low_ref, f32[4,40,128]{2,1,0:T(8,128)S(1)} %collective-permute-done.5.high_ref, bf16[1536,64]{1,0:T(8,128)(2,1)S(1)} %get-tuple-element.15.mid_ref, ...), custom_call_target="tpu_custom_call" | custom-call | tf_op jit(solution)/shard_map/forces/pallas_call | solution.py:496
  (3 shorter events, 0.0 us)
Async XLA Ops:
  1.4 0.7 copy-start
  2.8 23.0 %collective-permute-start = (f32[3,2,1,128]{3,2,1,0:T(1,128)S(1)}, f32[3,2,1,128]{3,2,1,0:T(1,128)S(1)}, u32[]{:S(2)}, u32[]{:S(2)}) collective-permute-start(f32[3,2,1,128]{3,2,1,0:T(1,128)S(1)} %get-tuple-element.30), channel_id=1, source_target_pairs={{0,32},{32,64},{64,96},{96,128},{128,160},{160,192},{192,224},{224... | collective-permute-start | bytes 9224 | tf_op jit(solution)/shard_map/ppermute | solution.py:517
  6.3 20.8 %collective-permute-start.1 = (f32[3,2,1,128]{3,2,1,0:T(1,128)S(1)}, f32[3,2,1,128]{3,2,1,0:T(1,128)S(1)}, u32[]{:S(2)}, u32[]{:S(2)}) collective-permute-start(f32[3,2,1,128]{3,2,1,0:T(1,128)S(1)} %get-tuple-element.31), channel_id=1, source_target_pairs={{0,992},{32,0},{64,32},{96,64},{128,96},{160,128},{192,160},{224,1... | collective-permute-start | bytes 9224 | tf_op jit(solution)/shard_map/ppermute | solution.py:518
  27.2 10.6 %collective-permute-start.3 = (f32[3,1,10,128]{3,2,1,0:T(8,128)S(1)}, f32[3,1,10,128]{3,2,1,0:T(8,128)S(1)}, u32[]{:S(2)}, u32[]{:S(2)}) collective-permute-start(f32[3,1,10,128]{3,2,1,0:T(8,128)S(1)} %get-tuple-element.28), channel_id=1, source_target_pairs={{0,24},{8,0},{16,8},{24,16},{1,25},{9,1},{17,9},{25,17},{2,26},{10... | collective-permute-start | bytes 46088 | tf_op jit(solution)/shard_map/ppermute | solution.py:521
  29.9 7.8 %collective-permute-start.2 = (f32[3,1,10,128]{3,2,1,0:T(8,128)S(1)}, f32[3,1,10,128]{3,2,1,0:T(8,128)S(1)}, u32[]{:S(2)}, u32[]{:S(2)}) collective-permute-start(f32[3,1,10,128]{3,2,1,0:T(8,128)S(1)} %get-tuple-element.29), channel_id=1, source_target_pairs={{0,8},{8,16},{16,24},{24,0},{1,9},{9,17},{17,25},{25,1},{2,10},{10... | collective-permute-start | bytes 46088 | tf_op jit(solution)/shard_map/ppermute | solution.py:520
  42.8 5.3 %collective-permute-start.5 = (f32[4,40,128]{2,1,0:T(8,128)S(1)}, f32[4,40,128]{2,1,0:T(8,128)S(1)}, u32[]{:S(2)}, u32[]{:S(2)}) collective-permute-start(f32[4,40,128]{2,1,0:T(8,128)S(1)} %get-tuple-element.18.plane_ref), channel_id=1, source_target_pairs={{0,7},{1,0},{2,1},{3,2},{4,3},{5,4},{6,5},{7,6},{8,15},{9,8},{10,9... | collective-permute-start | bytes 245768 | tf_op jit(solution)/shard_map/ppermute | solution.py:525
  46.0 7.6 %collective-permute-start.4 = (f32[4,40,128]{2,1,0:T(8,128)S(1)}, f32[4,40,128]{2,1,0:T(8,128)S(1)}, u32[]{:S(2)}, u32[]{:S(2)}) collective-permute-start(f32[4,40,128]{2,1,0:T(8,128)S(1)} %get-tuple-element.18.plane_ref), channel_id=1, source_target_pairs={{0,1},{1,2},{2,3},{3,4},{4,5},{5,6},{6,7},{7,0},{8,9},{9,10},{10,1... | collective-permute-start | bytes 245768 | tf_op jit(solution)/shard_map/ppermute | solution.py:524

commit v3 on v2

--- a/solution.py
+++ b/solution.py
@@ -19,7 +19,6 @@
 USES = ((0, (0,)), (1, (0, 1)), (2, (0,)), (3, (1,)))
 TIERS = (80, 96, S)
 OWN = 16
-ROLL = 80
 VMEM_LIMIT = 24 * 2**20
 F32 = jnp.float32
 BF16 = jnp.bfloat16
@@ -78,18 +77,28 @@
     return out + list(split3(1.0 - 4.0 * norm)) + [one, one, one] + [zero] * 8
 
 
-def build_far(t_ref, far_refs, kinds, rows=S):
+def build_far(t_ref, far_refs, rows=S):
+    low_half = lax.broadcasted_iota(jnp.int32, (rows, 2 * TERMS), 1) < TERMS
+
     def step(z, carry):
-        for kind, far_ref in zip(kinds, far_refs):
-            ya, yb = KINDS[kind]
+        sides = []
+        for y in (0, 2):
             both = jnp.concatenate(
-                [get_terms(t_ref, ya * NZR + z, TERMS), get_terms(t_ref, yb * NZR + z, TERMS)], 0
+                [get_terms(t_ref, y * NZR + z, TERMS), get_terms(t_ref, (y + 1) * NZR + z, TERMS)],
+                0,
             )
-            at = pl.multiple_of((z + 1) * S, S)
-            far_ref[pl.ds(at, rows), :] = both.T[:rows].astype(BF16)
+            sides.append(both.T[:rows])
+        at = pl.multiple_of((z + 1) * S, S)
+        for far_ref, first, second in zip(far_refs, (0, 1, 1, 0), (0, 0, 1, 1)):
+            if far_ref is None:
+                continue
+            value = sides[first]
+            if first != second:
+                value = jnp.where(low_half, sides[first], sides[second])
+            far_ref[pl.ds(at, rows), :] = value.astype(BF16)
         return carry
 
-    lax.fori_loop(0, NZR, step, 0)
+    lax.fori_loop(0, NZR, step, 0, unroll=5)
 
 
 def build_own(t_ref, own_ref, pair):
@@ -99,12 +108,14 @@
     def step(z, carry):
         a = get_terms(t_ref, ya * NZR + z, TERMS)
         b = get_terms(t_ref, yb * NZR + z, TERMS)
-        block = jnp.concatenate([jnp.concatenate([a, zero], 1), jnp.concatenate([zero, b], 1)], 0)
+        a = jnp.concatenate([a, zero], 1).astype(BF16)
+        b = jnp.concatenate([zero, b], 1).astype(BF16)
         at = pl.multiple_of((z + 1) * 2 * TERMS, 2 * TERMS)
-        own_ref[pl.ds(at, 2 * TERMS), :] = block.astype(BF16)
+        own_ref[0, pl.ds(at, 2 * TERMS), :] = jnp.concatenate([a, b], 0)
+        own_ref[1, pl.ds(at, 2 * TERMS), :] = jnp.concatenate([b, a], 0)
         return carry
 
-    lax.fori_loop(0, NZR, step, 0)
+    lax.fori_loop(0, NZR, step, 0, unroll=5)
 
 
 def empty_ends(ref, size):
@@ -120,18 +131,32 @@
     return far_ref[pl.ds(pl.multiple_of(slot * S, S), rows), :]
 
 
-def own_block(own_ref, slot):
-    return own_ref[pl.ds(pl.multiple_of(slot * 2 * TERMS, 2 * TERMS), 2 * TERMS), :]
+def own_block(own_ref, slot, kind):
+    at = pl.multiple_of(slot * 2 * TERMS, 2 * TERMS)
+    return own_ref[1 if kind == 1 else 0, pl.ds(at, 2 * TERMS), :]
 
 
 def closeness(rows, block):
     return jnp.maximum(jnp.dot(rows, block, preferred_element_type=F32), 0.0)
 
 
-def sort_kernel(pos_ref, counts_ref, own_ref, rank_ref, t_ref):
+def sort_kernel(pos_hbm, counts_hbm, own_ref, rank_ref, t_ref, pos_ref, counts_ref, sem_p, sem_c):
+    copy_p = pltpu.make_async_copy(pos_hbm, pos_ref, sem_p)
+    copy_c = pltpu.make_async_copy(counts_hbm, counts_ref, sem_c)
+    copy_p.start()
+    copy_c.start()
+    copy_p.wait()
+    copy_c.wait()
     lane = lax.broadcasted_iota(jnp.int32, (OWN, S), 1)
-    occupied = lane < counts_ref[...]
-    comps = [jnp.where(occupied, pos_ref[c], SENTINEL) for c in range(3)]
+    row = lax.broadcasted_iota(jnp.int32, (OWN, S), 0)
+    held = jnp.zeros((OWN, S), jnp.int32)
+    for cell in range(OWN):
+        held = jnp.where(row == cell, counts_ref[0, cell // 8, cell % 8], held)
+    occupied = lane < held
+    comps = [
+        jnp.where(occupied, jnp.concatenate([pos_ref[c, 0, 0], pos_ref[c, 0, 1]], 0), SENTINEL)
+        for c in range(3)
+    ]
     low = occupied & (comps[0] < 0.5)
     high = occupied & (comps[0] >= 0.5)
     up_to = lax.broadcasted_iota(jnp.int32, (S, S), 0) <= lax.broadcasted_iota(
@@ -163,13 +188,12 @@
 
 
 def row_sums(z, far_refs, kinds, own_ref, pair, rho, quart):
-    block = own_block(own_ref, z + 1)
     row = lax.broadcasted_iota(jnp.int32, (S, 2 * S), 0)
     lane = lax.broadcasted_iota(jnp.int32, (S, 2 * S), 1)
     itself = (row == lane) | (row + S == lane)
     for kind, far_ref in zip(kinds, far_refs):
         for dz in (-1, 0, 1):
-            weight = closeness(far_rows(far_ref, z + 1 + dz), block)
+            weight = closeness(far_rows(far_ref, z + 1 + dz), own_block(own_ref, z + 1, kind))
             square = weight * weight
             if dz == 0 and KINDS[kind] == PAIRS[pair]:
                 square = jnp.where(itself, 0.0, square)
@@ -186,9 +210,10 @@
             whole_ref[c, y * 3 * NZR : (y * 3 + 1) * NZR, :] = jnp.zeros((NZR, S), F32)
     coords = coordinates([whole_ref[c] for c in range(3)], 0.0)
     empty_ends(far_ref, S)
-    empty_ends(own_ref, 2 * TERMS)
+    empty_ends(own_ref.at[0], 2 * TERMS)
+    empty_ends(own_ref.at[1], 2 * TERMS)
     put_terms(t_ref, far_terms(coords))
-    build_far(t_ref, [far_ref], [1])
+    build_far(t_ref, [None, far_ref, None, None])
     put_terms(t_ref, own_terms(coords))
     build_own(t_ref, own_ref, 0)
     zero = jnp.zeros((8, 2 * S), F32)
@@ -199,7 +224,7 @@
         sums_ref[pl.ds(NZR + z, 1), :] = quart
         return carry
 
-    lax.fori_loop(0, NZR, step, 0)
+    lax.fori_loop(0, NZR, step, 0, unroll=5)
 
 
 def plane_kernel(
@@ -225,9 +250,10 @@
     coords = coordinates([plane_ref[c] for c in range(3)], 0.0)
     for ref in (far_a_ref, far_b_ref, far_c_ref):
         empty_ends(ref, S)
-    empty_ends(own_halo_ref, 2 * TERMS)
+    empty_ends(own_halo_ref.at[0], 2 * TERMS)
+    empty_ends(own_halo_ref.at[1], 2 * TERMS)
     put_terms(t_ref, far_terms(coords))
-    build_far(t_ref, [far_a_ref, far_b_ref, far_c_ref], [0, 2, 3])
+    build_far(t_ref, [far_a_ref, None, far_b_ref, far_c_ref])
     put_terms(t_ref, own_terms(coords))
     build_own(t_ref, own_halo_ref, 1)
     zero = jnp.zeros((8, 2 * S), F32)
@@ -245,7 +271,7 @@
         plane_ref[3, pl.ds(3 * NZR + z, 1), :] = rho[:, S:]
         return carry
 
-    lax.fori_loop(0, NZR, step, 0)
+    lax.fori_loop(0, NZR, step, 0, unroll=5)
 
 
 def column(row, rows=S):
@@ -276,44 +302,45 @@
     done_ref,
 ):
     lane = lax.broadcasted_iota(jnp.int32, (CELLS, S), 1)
-    for c in range(4):
-        rolled_ref[c] = pltpu.roll(low_ref[c], ROLL, 1)
-    x_low, x_high = rolled_ref[0], high_ref[0]
-    last = jnp.maximum(
-        jnp.where((x_low > 0.5) & (x_low < 2.0), lane, -1),
-        jnp.where(x_high < 0.5, lane, -1),
-    )
-    needed = jnp.max(last) + 1
+    x_low, x_high = low_ref[0], high_ref[0]
+    rows_used = jnp.maximum(
+        jnp.where((x_low > 0.5) & (x_low < 2.0), S - lane, 0),
+        jnp.where(x_high < 0.5, lane + 1, 0),
+    )
+    needed = jnp.max(rows_used)
     own_pairs = (own_ref, own_halo_ref)
     far0 = (far_a_ref, mid_ref, far_b_ref)
     sides = (rolled_ref, high_ref)
     rho_sum_ref[...] = jnp.zeros(rho_sum_ref.shape, F32)
     quart_sum_ref[...] = jnp.zeros(quart_sum_ref.shape, F32)
 
-    planes = (rolled_ref, plane_ref, high_ref)
-    for plane in range(3):
-        local = [planes[plane][c] - 0.5 for c in range(3)]
-        high = [v.astype(BF16).astype(F32) for v in local]
-        rest = [v - h for v, h in zip(local, high)]
-        put_terms(
-            t_ref, high + [jnp.ones((CELLS, S), F32)] + rest + [jnp.zeros((CELLS, S), F32)]
-        )
-
-        def gather(z, carry, plane=plane):
-            for kind, (ya, yb) in enumerate(KINDS[:3]):
-                both = jnp.concatenate(
-                    [get_terms(t_ref, ya * NZR + z, 8), get_terms(t_ref, yb * NZR + z, 8)], 0
-                )
-                xyz_ref[plane, kind, pl.ds(pl.multiple_of(z * 16, 16), 16), :] = both.astype(BF16)
-            return carry
-
-        lax.fori_loop(0, NZR, gather, 0)
-
     def with_rows(count):
+        for c in range(4):
+            rolled_ref[c] = low_ref[c] if count == S else pltpu.roll(low_ref[c], count, 1)
+
+        planes = (rolled_ref, plane_ref, high_ref)
+        for plane in range(3):
+            local = [planes[plane][c] - 0.5 for c in range(3)]
+            high = [v.astype(BF16).astype(F32) for v in local]
+            rest = [v - h for v, h in zip(local, high)]
+            put_terms(
+                t_ref, high + [jnp.ones((CELLS, S), F32)] + rest + [jnp.zeros((CELLS, S), F32)]
+            )
+
+            def gather(z, carry, plane=plane):
+                for kind, (ya, yb) in enumerate(KINDS[:3]):
+                    both = jnp.concatenate(
+                        [get_terms(t_ref, ya * NZR + z, 8), get_terms(t_ref, yb * NZR + z, 8)], 0
+                    )
+                    xyz_ref[plane, kind, pl.ds(pl.multiple_of(z * 16, 16), 16), :] = both.astype(BF16)
+                return carry
+
+            lax.fori_loop(0, NZR, gather, 0, unroll=2)
+
         for p in range(2):
             coords = coordinates([sides[p][c] for c in range(3)], (-1.0, 1.0)[p])
             put_terms(t_ref, far_terms(coords))
-            build_far(t_ref, [far_ref.at[p, k] for k in range(4)], range(4), count)
+            build_far(t_ref, [far_ref.at[p, k] for k in range(4)], count)
 
         def cross(z, carry):
             for p in range(2):
@@ -323,7 +350,7 @@
                     total = None
                     for dz in (-1, 0, 1):
                         for pair in pairs:
-                            weight = closeness(rows, own_block(own_pairs[pair], z + 1 + dz))
+                            weight = closeness(rows, own_block(own_pairs[pair], z + 1 + dz, kind))
                             square = weight * weight
                             total = square if total is None else total + square
                             at = pl.ds(pl.multiple_of((z + 1 + dz) * 8, 8), 8)
@@ -340,7 +367,7 @@
                     embed_ref[2 * p, pl.ds(at, count), :] = 2.5 * lax.rsqrt(rho + 1.0)
             return carry
 
-        lax.fori_loop(0, NZR, cross, 0)
+        lax.fori_loop(0, NZR, cross, 0, unroll=2)
 
         def finish(z, carry):
             for pair, ys in enumerate(PAIRS):
@@ -354,14 +381,13 @@
                     embed_ref[1, pl.ds(cell_at, S), :] = column(slope)
             return carry
 
-        lax.fori_loop(0, NZR, finish, 0)
+        lax.fori_loop(0, NZR, finish, 0, unroll=5)
 
         def push(i, carry):
             z = i + 1
             rho_at = pl.ds(pl.multiple_of((z + 1) * 8, 8), 8)
             rho_both = jnp.sum(rho_sum_ref[0, rho_at, :], 0, keepdims=True)
             quart_both = jnp.sum(quart_sum_ref[rho_at, :], 0, keepdims=True)
-            block = own_block(own_ref, z + 1)
             own = 1.0 + jnp.concatenate(
                 [row_ref[pl.ds(NZR + z, 1), :], row_ref[pl.ds(2 * NZR + z, 1), :]], 1
             )
@@ -376,7 +402,7 @@
                             rows = far_rows(far0[kind], z + 1 + dz)
                         else:
                             rows = far_rows(far_ref.at[(dx + 1) // 2, kind], z + 1 + dz, count)
-                        weight = closeness(rows, block)
+                        weight = closeness(rows, own_block(own_ref, z + 1, kind))
                         slopes = jnp.concatenate(
                             [
                                 embed_ref[
@@ -426,7 +452,7 @@
                     )
             return carry
 
-        lax.fori_loop(0, NZR - 2, push, 0)
+        lax.fori_loop(0, NZR - 2, push, 0, unroll=2)
 
     floor = 0
     for count in TIERS:
@@ -453,24 +479,35 @@
     return [(i, (i + step) % count) for i in range(count)]
 
 
-def kernel_call(body, outs, scratch, name):
+def kernel_call(body, outs, scratch, name, **specs):
     return pl.pallas_call(
         body,
+        **specs,
         out_shape=tuple(jax.ShapeDtypeStruct(shape, dtype) for shape, dtype in outs),
-        scratch_shapes=[pltpu.VMEM(shape, dtype) for shape, dtype in scratch],
+        scratch_shapes=[pltpu.VMEM(*s) if isinstance(s, tuple) else s for s in scratch],
         compiler_params=pltpu.CompilerParams(vmem_limit_bytes=VMEM_LIMIT),
         name=name,
     )
 
 
 FAR = ((SLOTS * S, 2 * TERMS), BF16)
-OWN_BLOCKS = ((SLOTS * 2 * TERMS, 2 * S), BF16)
+OWN_BLOCKS = ((2, SLOTS * 2 * TERMS, 2 * S), BF16)
 TERM_ROWS = ((TERMS * CELLS, S), F32)
 
 
 def sort_cells(positions, counts):
     return kernel_call(
-        sort_kernel, [((3, OWN, S), F32), ((OWN, S), F32)], [((16 * OWN, S), F32)], "sort"
+        sort_kernel,
+        [((3, OWN, S), F32), ((OWN, S), F32)],
+        [
+            ((16 * OWN, S), F32),
+            ((3, 1, 2, 8, S), F32),
+            pltpu.SMEM((1, 2, 8), jnp.int32),
+            pltpu.SemaphoreType.DMA(()),
+            pltpu.SemaphoreType.DMA(()),
+        ],
+        "sort",
+        in_specs=[pl.BlockSpec(memory_space=pltpu.HBM)] * 2,
     )(positions, counts)
 
 
@@ -512,7 +549,9 @@
 
 
 def per_device(positions, counts):
-    sorted_own, rank = sort_cells(positions.reshape(3, OWN, S), counts.reshape(OWN, 1))
+    positions = pltpu.with_memory_space_constraint(positions, pltpu.HBM)
+    counts = pltpu.with_memory_space_constraint(counts, pltpu.HBM)
+    sorted_own, rank = sort_cells(positions, counts)
     cells = sorted_own.reshape(3, 2, 8, S)
     behind = lax.ppermute(cells[:, :, 7:8], "gz", ring("gz", 1))
     ahead = lax.ppermute(cells[:, :, 0:1], "gz", ring("gz", -1))

time: 76.7 us -> 68.3 us (0.89)
  the two profiles are of different devices: /device:TPU:6 before, /device:TPU:56 now
where the time goes in v3:
time: 68.3 us; the launch traced here: 67.2 us
  starting transfers between devices  25 us (37%)
  Pallas kernels  22.8 us (33%)
  waiting for transfers between devices  18.6 us (27%)
  between operations  0.73 us (1%)
    pallas_call x1, Pallas kernels, finish_forces(): kernel_call(force_kernel, [((OWN, S), F32), ((3 * OWN, S), F32)], [TERM_R...  16.7 us
    ppermute x1, starting transfers between devices, per_device(): behind = lax.ppermute(cells[:, :, 7:8], 'gz', ring('gz', 1))  10.1 us
    ppermute x1, waiting for transfers between devices, per_device(): ahead = lax.ppermute(cells[:, :, 0:1], 'gz', ring('gz', -1))  9.57 us
    ppermute x1, waiting for transfers between devices, per_device(): low = lax.ppermute(plane, 'gx', ring('gx', 1))  5.54 us
    ppermute x1, starting transfers between devices, per_device(): above = lax.ppermute(rows[:, 0:1], 'gy', ring('gy', -1))  4.67 us
    ppermute x1, starting transfers between devices, per_device(): high = lax.ppermute(plane, 'gx', ring('gx', -1))  4.46 us
    ppermute x1, waiting for transfers between devices, per_device(): below = lax.ppermute(rows[:, 1:2], 'gy', ring('gy', 1))  3.41 us
    pallas_call x1, Pallas kernels, plane_sums(): kernel_call(plane_kernel, [((4, CELLS, S), F32), FAR, FAR, OWN_BLOCKS, ((...  3.13 us
  transfers between devices with their start and end apart: 6, of which 4 were waited for; matrix products, arithmetic and copies ran while one was open for 0% of the time, Pallas kernels for 2%

profile of v3, /device:TPU:56, one launch (start us, length us, event | category | flops | bytes accessed | tf_op | source)
XLA Modules:
  0.0 67.2 jit_solution(9083930082727410920)
XLA Ops:
  0.6 1.4 %sort.1 = (f32[3,16,128]{2,1,0:T(8,128)S(1)}, f32[16,128]{1,0:T(8,128)S(1)}) custom-call(f32[3,1,2,8,128]{4,3,2,1,0:T(8,128)} %pos_hbm.1, s32[1,2,8]{2,1,0:T(2,128)} %counts_hbm.1), custom_call_target="tpu_custom_call" | custom-call | tf_op jit(solution)/shard_map/sort/pallas_call | solution.py:499
  2.1 10.1 %collective-permute-start = (f32[3,2,1,128]{3,2,1,0:T(1,128)S(1)}, f32[3,2,1,128]{3,2,1,0:T(1,128)S(1)}, u32[]{:S(2)}, u32[]{:S(2)}) collective-permute-start(f32[3,2,1,128]{3,2,1,0:T(1,128)S(1)} %get-tuple-element.30), channel_id=1, source_target_pairs={{0,32},{32,64},{64,96},{96,128},{128,160},{160,192},{192,224},{224... | collective-permute-start | bytes 9224 | tf_op jit(solution)/shard_map/ppermute | solution.py:556
  12.2 1.9 %collective-permute-start.1 = (f32[3,2,1,128]{3,2,1,0:T(1,128)S(1)}, f32[3,2,1,128]{3,2,1,0:T(1,128)S(1)}, u32[]{:S(2)}, u32[]{:S(2)}) collective-permute-start(f32[3,2,1,128]{3,2,1,0:T(1,128)S(1)} %get-tuple-element.31), channel_id=1, source_target_pairs={{0,992},{32,0},{64,32},{96,64},{128,96},{160,128},{192,160},{224,1... | collective-permute-start | bytes 9224 | tf_op jit(solution)/shard_map/ppermute | solution.py:557
  14.1 0.0 collective-permute-done
  14.2 9.6 %collective-permute-done.1 = f32[3,2,1,128]{3,2,1,0:T(1,128)S(1)} collective-permute-done((f32[3,2,1,128]{3,2,1,0:T(1,128)S(1)}, f32[3,2,1,128]{3,2,1,0:T(1,128)S(1)}, u32[]{:S(2)}, u32[]{:S(2)}) %collective-permute-start.1) | collective-permute-done | bytes 3104 | tf_op jit(solution)/shard_map/ppermute | solution.py:557
  23.8 4.7 %collective-permute-start.3 = (f32[3,1,10,128]{3,2,1,0:T(8,128)S(1)}, f32[3,1,10,128]{3,2,1,0:T(8,128)S(1)}, u32[]{:S(2)}, u32[]{:S(2)}) collective-permute-start(f32[3,1,10,128]{3,2,1,0:T(8,128)S(1)} %get-tuple-element.28), channel_id=1, source_target_pairs={{0,24},{8,0},{16,8},{24,16},{1,25},{9,1},{17,9},{25,17},{2,26},{10... | collective-permute-start | bytes 46088 | tf_op jit(solution)/shard_map/ppermute | solution.py:560
  28.4 1.9 %collective-permute-start.2 = (f32[3,1,10,128]{3,2,1,0:T(8,128)S(1)}, f32[3,1,10,128]{3,2,1,0:T(8,128)S(1)}, u32[]{:S(2)}, u32[]{:S(2)}) collective-permute-start(f32[3,1,10,128]{3,2,1,0:T(8,128)S(1)} %get-tuple-element.29), channel_id=1, source_target_pairs={{0,8},{8,16},{16,24},{24,0},{1,9},{9,17},{17,25},{25,1},{2,10},{10... | collective-permute-start | bytes 46088 | tf_op jit(solution)/shard_map/ppermute | solution.py:559
  30.4 1.6 %rows.1 = (bf16[1536,64]{1,0:T(8,128)(2,1)S(1)}, bf16[2,768,256]{2,1,0:T(8,128)(2,1)S(1)}, f32[20,256]{1,0:T(8,128)S(1)}) custom-call(f32[3,2,10,128]{3,2,1,0:T(8,128)S(1)} %pad_maximum_fusion.pos_ref), custom_call_target="tpu_custom_call" | custom-call | tf_op jit(solution)/shard_map/rows/pallas_call | solution.py:515
  31.9 0.0 collective-permute-done.3.above_ref
  31.9 3.4 %collective-permute-done.2.below_ref = f32[3,1,10,128]{3,2,1,0:T(8,128)S(1)} collective-permute-done((f32[3,1,10,128]{3,2,1,0:T(8,128)S(1)}, f32[3,1,10,128]{3,2,1,0:T(8,128)S(1)}, u32[]{:S(2)}, u32[]{:S(2)}) %collective-permute-start.2) | collective-permute-done | bytes 15392 | tf_op jit(solution)/shard_map/ppermute | solution.py:559
  35.4 3.1 %plane.1 = (f32[4,40,128]{2,1,0:T(8,128)S(1)}, bf16[1536,64]{1,0:T(8,128)(2,1)S(1)}, bf16[1536,64]{1,0:T(8,128)(2,1)S(1)}, bf16[2,768,256]{2,1,0:T(8,128)(2,1)S(1)}, f32[20,128]{1,0:T(8,128)S(1)}) custom-call(f32[3,2,10,128]{3,2,1,0:T(8,128)S(1)} %pad_maximum_fusion.pos_ref, f32[3,1,10,128]{3,2,1,0:T(8,128)S(1)} %collective-permute-done.2.below_ref, ...), custom_call_target="tpu_custom_call" | custom-call | tf_op jit(solution)/shard_map/plane/pallas_call | solution.py:524
  38.5 4.5 %collective-permute-start.5 = (f32[4,40,128]{2,1,0:T(8,128)S(1)}, f32[4,40,128]{2,1,0:T(8,128)S(1)}, u32[]{:S(2)}, u32[]{:S(2)}) collective-permute-start(f32[4,40,128]{2,1,0:T(8,128)S(1)} %get-tuple-element.18.plane_ref), channel_id=1, source_target_pairs={{0,7},{1,0},{2,1},{3,2},{4,3},{5,4},{6,5},{7,6},{8,15},{9,8},{10,9... | collective-permute-start | bytes 245768 | tf_op jit(solution)/shard_map/ppermute | solution.py:564
  43.0 1.9 %collective-permute-start.4 = (f32[4,40,128]{2,1,0:T(8,128)S(1)}, f32[4,40,128]{2,1,0:T(8,128)S(1)}, u32[]{:S(2)}, u32[]{:S(2)}) collective-permute-start(f32[4,40,128]{2,1,0:T(8,128)S(1)} %get-tuple-element.18.plane_ref), channel_id=1, source_target_pairs={{0,1},{1,2},{2,3},{3,4},{4,5},{5,6},{6,7},{7,0},{8,9},{9,10},{10,1... | collective-permute-start | bytes 245768 | tf_op jit(solution)/shard_map/ppermute | solution.py:563
  44.9 0.1 collective-permute-done.5.high_ref
  45.0 5.5 %collective-permute-done.4.low_ref = f32[4,40,128]{2,1,0:T(8,128)S(1)} collective-permute-done((f32[4,40,128]{2,1,0:T(8,128)S(1)}, f32[4,40,128]{2,1,0:T(8,128)S(1)}, u32[]{:S(2)}, u32[]{:S(2)}) %collective-permute-start.4) | collective-permute-done | bytes 81952 | tf_op jit(solution)/shard_map/ppermute | solution.py:563
  50.5 16.7 %forces.1 = (f32[16,128]{1,0:T(8,128)}, f32[48,128]{1,0:T(8,128)}) custom-call(f32[4,40,128]{2,1,0:T(8,128)S(1)} %get-tuple-element.18.plane_ref, f32[4,40,128]{2,1,0:T(8,128)S(1)} %collective-permute-done.4.low_ref, f32[4,40,128]{2,1,0:T(8,128)S(1)} %collective-permute-done.5.high_ref, bf16[1536,64]{1,0:T(8,128)(2,1)S(1)} %get-tuple-element.15.mid_ref, ...), custom_call_target="tpu_custom_call" | custom-call | tf_op jit(solution)/shard_map/forces/pallas_call | solution.py:533
  (3 shorter events, 0.0 us)
Async XLA Ops:
  2.1 12.1 %collective-permute-start = (f32[3,2,1,128]{3,2,1,0:T(1,128)S(1)}, f32[3,2,1,128]{3,2,1,0:T(1,128)S(1)}, u32[]{:S(2)}, u32[]{:S(2)}) collective-permute-start(f32[3,2,1,128]{3,2,1,0:T(1,128)S(1)} %get-tuple-element.30), channel_id=1, source_target_pairs={{0,32},{32,64},{64,96},{96,128},{128,160},{160,192},{192,224},{224... | collective-permute-start | bytes 9224 | tf_op jit(solution)/shard_map/ppermute | solution.py:556
  12.2 11.5 %collective-permute-start.1 = (f32[3,2,1,128]{3,2,1,0:T(1,128)S(1)}, f32[3,2,1,128]{3,2,1,0:T(1,128)S(1)}, u32[]{:S(2)}, u32[]{:S(2)}) collective-permute-start(f32[3,2,1,128]{3,2,1,0:T(1,128)S(1)} %get-tuple-element.31), channel_id=1, source_target_pairs={{0,992},{32,0},{64,32},{96,64},{128,96},{160,128},{192,160},{224,1... | collective-permute-start | bytes 9224 | tf_op jit(solution)/shard_map/ppermute | solution.py:557
  23.8 8.2 %collective-permute-start.3 = (f32[3,1,10,128]{3,2,1,0:T(8,128)S(1)}, f32[3,1,10,128]{3,2,1,0:T(8,128)S(1)}, u32[]{:S(2)}, u32[]{:S(2)}) collective-permute-start(f32[3,1,10,128]{3,2,1,0:T(8,128)S(1)} %get-tuple-element.28), channel_id=1, source_target_pairs={{0,24},{8,0},{16,8},{24,16},{1,25},{9,1},{17,9},{25,17},{2,26},{10... | collective-permute-start | bytes 46088 | tf_op jit(solution)/shard_map/ppermute | solution.py:560
  28.4 6.9 %collective-permute-start.2 = (f32[3,1,10,128]{3,2,1,0:T(8,128)S(1)}, f32[3,1,10,128]{3,2,1,0:T(8,128)S(1)}, u32[]{:S(2)}, u32[]{:S(2)}) collective-permute-start(f32[3,1,10,128]{3,2,1,0:T(8,128)S(1)} %get-tuple-element.29), channel_id=1, source_target_pairs={{0,8},{8,16},{16,24},{24,0},{1,9},{9,17},{17,25},{25,1},{2,10},{10... | collective-permute-start | bytes 46088 | tf_op jit(solution)/shard_map/ppermute | solution.py:559
  38.5 6.5 %collective-permute-start.5 = (f32[4,40,128]{2,1,0:T(8,128)S(1)}, f32[4,40,128]{2,1,0:T(8,128)S(1)}, u32[]{:S(2)}, u32[]{:S(2)}) collective-permute-start(f32[4,40,128]{2,1,0:T(8,128)S(1)} %get-tuple-element.18.plane_ref), channel_id=1, source_target_pairs={{0,7},{1,0},{2,1},{3,2},{4,3},{5,4},{6,5},{7,6},{8,15},{9,8},{10,9... | collective-permute-start | bytes 245768 | tf_op jit(solution)/shard_map/ppermute | solution.py:564
  43.0 7.6 %collective-permute-start.4 = (f32[4,40,128]{2,1,0:T(8,128)S(1)}, f32[4,40,128]{2,1,0:T(8,128)S(1)}, u32[]{:S(2)}, u32[]{:S(2)}) collective-permute-start(f32[4,40,128]{2,1,0:T(8,128)S(1)} %get-tuple-element.18.plane_ref), channel_id=1, source_target_pairs={{0,1},{1,2},{2,3},{3,4},{4,5},{5,6},{6,7},{7,0},{8,9},{9,10},{10,1... | collective-permute-start | bytes 245768 | tf_op jit(solution)/shard_map/ppermute | solution.py:563

commit v4 on v3

--- a/solution.py
+++ b/solution.py
@@ -187,20 +187,73 @@
             ) + moved[3 * c + 2 : 3 * c + 3]
 
 
-def row_sums(z, far_refs, kinds, own_ref, pair, rho, quart):
+def itself():
     row = lax.broadcasted_iota(jnp.int32, (S, 2 * S), 0)
     lane = lax.broadcasted_iota(jnp.int32, (S, 2 * S), 1)
-    itself = (row == lane) | (row + S == lane)
+    return (row == lane) | (row + S == lane)
+
+
+def row_sums(z, far_refs, kinds, own_ref, pair):
+    rho = jnp.zeros((8, 2 * S), F32)
     for kind, far_ref in zip(kinds, far_refs):
         for dz in (-1, 0, 1):
             weight = closeness(far_rows(far_ref, z + 1 + dz), own_block(own_ref, z + 1, kind))
             square = weight * weight
             if dz == 0 and KINDS[kind] == PAIRS[pair]:
-                square = jnp.where(itself, 0.0, square)
+                square = jnp.where(itself(), 0.0, square)
             rho = rho + fold(square)
-            if pair == 0:
-                quart = quart + fold(square * square)
-    return jnp.sum(rho, 0, keepdims=True), jnp.sum(quart, 0, keepdims=True)
+    return jnp.sum(rho, 0, keepdims=True)
+
+
+def put_gathered(t_ref, xyz_refs, terms):
+    put_terms(t_ref, terms)
+
+    def gather(z, carry):
+        for kind, (ya, yb) in enumerate(KINDS[:3]):
+            both = jnp.concatenate(
+                [get_terms(t_ref, ya * NZR + z, 8), get_terms(t_ref, yb * NZR + z, 8)], 0
+            )
+            xyz_refs[kind, pl.ds(pl.multiple_of(z * 16, 16), 16), :] = both.astype(BF16)
+        return carry
+
+    lax.fori_loop(0, NZR, gather, 0, unroll=5)
+
+
+def split2(value):
+    high = value.astype(BF16)
+    return high, (value - high.astype(F32)).astype(BF16)
+
+
+def local_terms(comps):
+    local = [c - 0.5 for c in comps]
+    high = [v.astype(BF16).astype(F32) for v in local]
+    rest = [v - h for v, h in zip(local, high)]
+    return high + [jnp.ones((CELLS, S), F32)] + rest + [jnp.zeros((CELLS, S), F32)]
+
+
+def no_sums():
+    names = ("all", "x-", "x+", "y-", "y+", "z-", "z+")
+    return [{n: jnp.zeros((8, S), F32) for n in names} for _ in range(2)]
+
+
+def add_sums(sums, rows, limbs, offset):
+    both = sum(jnp.dot(rows, limb, preferred_element_type=F32) for limb in limbs)
+    keys = ["all"] + [a + "-0+"[d + 1] for a, d in zip("xyz", offset) if d]
+    for part_of, held in enumerate(sums):
+        for half in range(2):
+            at = part_of * 16 + half * 8
+            part = both[at : at + 8, half * S : half * S + S]
+            for key in keys:
+                held[half][key] = held[half][key] + part
+
+
+def resolve(acc):
+    both = {key: value[0:4] + value[4:8] for key, value in acc.items()}
+    out = [
+        both["all"][c : c + 1] + (both[a + "+"][3:4] - both[a + "-"][3:4])
+        for c, a in enumerate("xyz")
+    ]
+    return out + [both["all"][3:4]]
 
 
 def pair_row_kernel(pos_ref, far_ref, own_ref, sums_ref, t_ref, whole_ref):
@@ -216,12 +269,9 @@
     build_far(t_ref, [None, far_ref, None, None])
     put_terms(t_ref, own_terms(coords))
     build_own(t_ref, own_ref, 0)
-    zero = jnp.zeros((8, 2 * S), F32)
 
     def step(z, carry):
-        rho, quart = row_sums(z, [far_ref], [1], own_ref, 0, zero, zero)
-        sums_ref[pl.ds(z, 1), :] = rho
-        sums_ref[pl.ds(NZR + z, 1), :] = quart
+        sums_ref[pl.ds(z, 1), :] = row_sums(z, [far_ref], [1], own_ref, 0)
         return carry
 
     lax.fori_loop(0, NZR, step, 0, unroll=5)
@@ -238,7 +288,6 @@
     far_a_ref,
     far_b_ref,
     own_halo_ref,
-    quart_ref,
     t_ref,
     far_c_ref,
 ):
@@ -256,22 +305,62 @@
     build_far(t_ref, [far_a_ref, None, far_b_ref, far_c_ref])
     put_terms(t_ref, own_terms(coords))
     build_own(t_ref, own_halo_ref, 1)
-    zero = jnp.zeros((8, 2 * S), F32)
 
     def step(z, carry):
-        rho, quart = row_sums(z, [far_a_ref, far_b_ref], [0, 2], own_ref, 0, zero, zero)
-        rho = rho + sums_ref[pl.ds(z, 1), :]
-        quart = quart + sums_ref[pl.ds(NZR + z, 1), :]
+        rho = row_sums(z, [far_a_ref, far_b_ref], [0, 2], own_ref, 0) + sums_ref[pl.ds(z, 1), :]
         plane_ref[3, pl.ds(NZR + z, 1), :] = rho[:, :S]
         plane_ref[3, pl.ds(2 * NZR + z, 1), :] = rho[:, S:]
-        quart_ref[pl.ds(z, 1), :] = quart[:, :S]
-        quart_ref[pl.ds(NZR + z, 1), :] = quart[:, S:]
-        rho, _ = row_sums(z, [mid_ref, far_c_ref], [1, 3], own_halo_ref, 1, zero, zero)
+        rho = row_sums(z, [mid_ref, far_c_ref], [1, 3], own_halo_ref, 1)
         plane_ref[3, pl.ds(z, 1), :] = rho[:, :S]
         plane_ref[3, pl.ds(3 * NZR + z, 1), :] = rho[:, S:]
         return carry
 
     lax.fori_loop(0, NZR, step, 0, unroll=5)
+
+
+def inner_kernel(
+    plane_ref,
+    mid_ref,
+    far_a_ref,
+    far_b_ref,
+    own_ref,
+    top_ref,
+    low_ref,
+    cube_ref,
+    quart_ref,
+    xyz_ref,
+    t_ref,
+):
+    far0 = (far_a_ref, mid_ref, far_b_ref)
+    put_gathered(t_ref, xyz_ref, local_terms([plane_ref[c] for c in range(3)]))
+
+    def step(i, carry):
+        z = i + 1
+        cube = no_sums()
+        quart = jnp.zeros((8, 2 * S), F32)
+        for kind in range(3):
+            for dz in (-1, 0, 1):
+                weight = closeness(
+                    far_rows(far0[kind], z + 1 + dz), own_block(own_ref, z + 1, kind)
+                )
+                if kind == 1 and dz == 0:
+                    weight = jnp.where(itself(), 0.0, weight)
+                square = weight * weight
+                quart = quart + fold(square * square)
+                limbs = split2(weight)
+                at = pl.ds(pl.multiple_of((i * 9 + kind * 3 + dz + 1) * S, S), S)
+                top_ref[at, :] = limbs[0]
+                low_ref[at, :] = limbs[1]
+                rows = xyz_ref[kind, pl.ds(pl.multiple_of((z + dz) * 16, 16), 16), :]
+                add_sums([cube], rows, split2(square * weight), (0, kind - 1, dz))
+        quart = jnp.sum(quart, 0, keepdims=True)
+        for half in range(2):
+            for c, part in enumerate(resolve(cube[half])):
+                cube_ref[pl.ds((half * 4 + c) * 8 + i, 1), :] = part
+            quart_ref[pl.ds(half * 8 + i, 1), :] = quart[:, half * S : (half + 1) * S]
+        return carry
+
+    lax.fori_loop(0, NZR - 2, step, 0, unroll=2)
 
 
 def column(row, rows=S):
@@ -282,12 +371,13 @@
     plane_ref,
     low_ref,
     high_ref,
-    mid_ref,
-    far_a_ref,
-    far_b_ref,
     own_ref,
     own_halo_ref,
+    top_ref,
+    rest_ref,
+    cube_ref,
     quart_ref,
+    local_ref,
     rank_ref,
     energy_ref,
     forces_ref,
@@ -309,7 +399,6 @@
     )
     needed = jnp.max(rows_used)
     own_pairs = (own_ref, own_halo_ref)
-    far0 = (far_a_ref, mid_ref, far_b_ref)
     sides = (rolled_ref, high_ref)
     rho_sum_ref[...] = jnp.zeros(rho_sum_ref.shape, F32)
     quart_sum_ref[...] = jnp.zeros(quart_sum_ref.shape, F32)
@@ -318,24 +407,8 @@
         for c in range(4):
             rolled_ref[c] = low_ref[c] if count == S else pltpu.roll(low_ref[c], count, 1)
 
-        planes = (rolled_ref, plane_ref, high_ref)
-        for plane in range(3):
-            local = [planes[plane][c] - 0.5 for c in range(3)]
-            high = [v.astype(BF16).astype(F32) for v in local]
-            rest = [v - h for v, h in zip(local, high)]
-            put_terms(
-                t_ref, high + [jnp.ones((CELLS, S), F32)] + rest + [jnp.zeros((CELLS, S), F32)]
-            )
-
-            def gather(z, carry, plane=plane):
-                for kind, (ya, yb) in enumerate(KINDS[:3]):
-                    both = jnp.concatenate(
-                        [get_terms(t_ref, ya * NZR + z, 8), get_terms(t_ref, yb * NZR + z, 8)], 0
-                    )
-                    xyz_ref[plane, kind, pl.ds(pl.multiple_of(z * 16, 16), 16), :] = both.astype(BF16)
-                return carry
-
-            lax.fori_loop(0, NZR, gather, 0, unroll=2)
+        for p in range(2):
+            put_gathered(t_ref, xyz_ref.at[2 * p], local_terms([sides[p][c] for c in range(3)]))
 
         for p in range(2):
             coords = coordinates([sides[p][c] for c in range(3)], (-1.0, 1.0)[p])
@@ -364,10 +437,10 @@
                     part = column(sides[p][3, pl.ds(y * NZR + z, 1), :], count)
                     rho = jnp.sum(across[y], 1, keepdims=True) + part
                     at = pl.multiple_of((y * NZR + z) * S, S)
-                    embed_ref[2 * p, pl.ds(at, count), :] = 2.5 * lax.rsqrt(rho + 1.0)
+                    embed_ref[p, pl.ds(at, count), :] = 2.5 * lax.rsqrt(rho + 1.0)
             return carry
 
-        lax.fori_loop(0, NZR, cross, 0, unroll=2)
+        lax.fori_loop(0, NZR, cross, 0, unroll=5)
 
         def finish(z, carry):
             for pair, ys in enumerate(PAIRS):
@@ -375,13 +448,14 @@
                 sums = jnp.sum(rho_sum_ref[pair, at, :], 0, keepdims=True)
                 for half, y in enumerate(ys):
                     rho = plane_ref[3, pl.ds(y * NZR + z, 1), :] + sums[:, half * S : half * S + S]
-                    slope = 2.5 * lax.rsqrt(rho + 1.0)
-                    row_ref[pl.ds(y * NZR + z, 1), :] = slope
-                    cell_at = pl.multiple_of((y * NZR + z) * S, S)
-                    embed_ref[1, pl.ds(cell_at, S), :] = column(slope)
+                    row_ref[pl.ds(y * NZR + z, 1), :] = 2.5 * lax.rsqrt(rho + 1.0)
             return carry
 
         lax.fori_loop(0, NZR, finish, 0, unroll=5)
+        slopes = row_ref[...]
+        weighted = [slopes * (plane_ref[c] - 0.5) for c in range(3)] + [slopes]
+        high = [v.astype(BF16).astype(F32) for v in weighted]
+        put_gathered(t_ref, xyz_ref.at[1], high + [v - h for v, h in zip(weighted, high)])
 
         def push(i, carry):
             z = i + 1
@@ -391,23 +465,33 @@
             own = 1.0 + jnp.concatenate(
                 [row_ref[pl.ds(NZR + z, 1), :], row_ref[pl.ds(2 * NZR + z, 1), :]], 1
             )
-            names = ("all", "x-", "x+", "y-", "y+", "z-", "z+")
-            sums = [{n: jnp.zeros((8, S), F32) for n in names} for _ in range(2)]
-            for dx in (-1, 0, 1):
-                used = S if dx == 0 else count
-                for dy in (-1, 0, 1):
-                    kind = dy + 1
+            sums, line = no_sums(), no_sums()
+            for dx in (0, -1, 1):
+                for kind in range(3):
                     for dz in (-1, 0, 1):
+                        xyz = xyz_ref[
+                            dx + 1, kind, pl.ds(pl.multiple_of((z + dz) * 16, 16), 16), :
+                        ]
+                        offset = (dx, kind - 1, dz)
                         if dx == 0:
-                            rows = far_rows(far0[kind], z + 1 + dz)
-                        else:
-                            rows = far_rows(far_ref.at[(dx + 1) // 2, kind], z + 1 + dz, count)
+                            at = pl.ds(pl.multiple_of((i * 9 + kind * 3 + dz + 1) * S, S), S)
+                            local = local_ref[
+                                kind, pl.ds(pl.multiple_of((z + dz) * 16, 16), 16), :
+                            ]
+                            add_sums(
+                                [sums, line],
+                                jnp.concatenate([xyz, local], 0),
+                                (top_ref[at, :], rest_ref[at, :]),
+                                offset,
+                            )
+                            continue
+                        rows = far_rows(far_ref.at[(dx + 1) // 2, kind], z + 1 + dz, count)
                         weight = closeness(rows, own_block(own_ref, z + 1, kind))
                         slopes = jnp.concatenate(
                             [
                                 embed_ref[
-                                    dx + 1,
-                                    pl.ds(pl.multiple_of((y * NZR + z + dz) * S, S), used),
+                                    (dx + 1) // 2,
+                                    pl.ds(pl.multiple_of((y * NZR + z + dz) * S, S), count),
                                     :,
                                 ]
                                 for y in KINDS[kind]
@@ -415,36 +499,21 @@
                             1,
                         )
                         factor = weight * ((own + slopes) - weight * weight)
-                        top = factor.astype(BF16)
-                        low = (factor - top.astype(F32)).astype(BF16)
-                        xyz = xyz_ref[
-                            dx + 1, kind, pl.ds(pl.multiple_of((z + dz) * 16, 16), 16), :
-                        ][:, :used]
-                        both = jnp.dot(xyz, top, preferred_element_type=F32) + jnp.dot(
-                            xyz, low, preferred_element_type=F32
-                        )
-                        keys = ["all"]
-                        keys += [a + "-0+"[d + 1] for a, d in zip("xyz", (dx, dy, dz)) if d]
-                        for half in range(2):
-                            part = both[half * 8 : half * 8 + 8, half * S : half * S + S]
-                            for key in keys:
-                                sums[half][key] = sums[half][key] + part
+                        add_sums([sums], xyz[:, :count], split2(factor), offset)
             for half in range(2):
                 y = half + 1
                 at = pl.ds(y * NZR + z, 1)
                 occupied = plane_ref[0, at, :] < 2.0
-                acc = sums[half]
-                weight_sum = acc["all"][3:4]
-                rho = plane_ref[3, at, :] + rho_both[:, half * S : (half + 1) * S]
-                quart = (
-                    quart_ref[pl.ds(half * NZR + z, 1), :]
-                    + quart_both[:, half * S : (half + 1) * S]
-                )
+                lanes = slice(half * S, (half + 1) * S)
+                moved = []
+                for c, (part, first) in enumerate(zip(resolve(sums[half]), resolve(line[half]))):
+                    cube = cube_ref[pl.ds((half * 4 + c) * 8 + i, 1), :]
+                    moved.append(part + (own[:, lanes] * first - cube))
+                rho = plane_ref[3, at, :] + rho_both[:, lanes]
+                quart = quart_ref[pl.ds(half * 8 + i, 1), :] + quart_both[:, lanes]
                 results = [-0.2 * jnp.sqrt(rho + 1.0) + 0.01 * (quart - 2.0 * rho)]
-                for c, axis in enumerate("xyz"):
-                    moved = acc[axis + "+"][3:4] - acc[axis + "-"][3:4]
-                    centre = acc["all"][c : c + 1] + acc["all"][c + 4 : c + 5]
-                    force = (centre + moved) - (plane_ref[c, at, :] - 0.5) * weight_sum
+                for c in range(3):
+                    force = moved[c] - (plane_ref[c, at, :] - 0.5) * moved[3]
                     results.append(0.64 * force)
                 for k, result in enumerate(results):
                     done_ref[pl.ds(k * OWN + half * 8 + i, 1), :] = jnp.where(
@@ -514,7 +583,7 @@
 def pair_row(rows):
     return kernel_call(
         pair_row_kernel,
-        [FAR, OWN_BLOCKS, ((2 * NZR, 2 * S), F32)],
+        [FAR, OWN_BLOCKS, ((NZR, 2 * S), F32)],
         [TERM_ROWS, ((3, CELLS, S), F32)],
         "rows",
     )(rows)
@@ -523,10 +592,25 @@
 def plane_sums(rows, below, above, mid, own, sums):
     return kernel_call(
         plane_kernel,
-        [((4, CELLS, S), F32), FAR, FAR, OWN_BLOCKS, ((2 * NZR, S), F32)],
+        [((4, CELLS, S), F32), FAR, FAR, OWN_BLOCKS],
         [TERM_ROWS, FAR],
         "plane",
     )(rows, below, above, mid, own, sums)
+
+
+def inner_sums(*operands):
+    return kernel_call(
+        inner_kernel,
+        [
+            ((8 * 9 * S, 2 * S), BF16),
+            ((8 * 9 * S, 2 * S), BF16),
+            ((8 * 8, S), F32),
+            ((OWN, S), F32),
+            ((3, NZR * 16, S), BF16),
+        ],
+        [TERM_ROWS],
+        "inner",
+    )(*operands)
 
 
 def finish_forces(*operands):
@@ -540,7 +624,7 @@
             ((3, 3, NZR * 16, S), BF16),
             ((2, SLOTS * 8, 2 * S), F32),
             ((SLOTS * 8, 2 * S), F32),
-            ((3, CELLS * S, S), F32),
+            ((2, CELLS * S, S), F32),
             ((CELLS, S), F32),
             ((4 * OWN, S), F32),
         ],
@@ -559,12 +643,11 @@
     below = lax.ppermute(rows[:, 1:2], "gy", ring("gy", 1))
     above = lax.ppermute(rows[:, 0:1], "gy", ring("gy", -1))
     mid, own, sums = pair_row(rows)
-    plane, far_a, far_b, own_halo, quart = plane_sums(rows, below, above, mid, own, sums)
+    plane, far_a, far_b, own_halo = plane_sums(rows, below, above, mid, own, sums)
     low = lax.ppermute(plane, "gx", ring("gx", 1))
     high = lax.ppermute(plane, "gx", ring("gx", -1))
-    energy, forces = finish_forces(
-        plane, low, high, mid, far_a, far_b, own, own_halo, quart, rank
-    )
+    inner = inner_sums(plane, mid, far_a, far_b, own)
+    energy, forces = finish_forces(plane, low, high, own, own_halo, *inner, rank)
     return (energy.reshape(1, 2, 8, S), forces.reshape(3, 1, 2, 8, S))
 
 

time: 68.3 us -> 67.4 us (0.987)
  the two profiles are of different devices: /device:TPU:56 before, /device:TPU:6 now
where the time goes in v4:
time: 67.4 us; the launch traced here: 67.7 us
  starting transfers between devices  36.2 us (54%)
  Pallas kernels  25.9 us (38%)
  waiting for transfers between devices  4.87 us (7%)
  between operations  0.75 us (1%)
    ppermute x1, starting transfers between devices, per_device(): ahead = lax.ppermute(cells[:, :, 0:1], 'gz', ring('gz', -1))  19.5 us
    pallas_call x1, Pallas kernels, finish_forces(): kernel_call(force_kernel, [((OWN, S), F32), ((3 * OWN, S), F32)], [TERM_R...  15.3 us
    ppermute x1, starting transfers between devices, per_device(): high = lax.ppermute(plane, 'gx', ring('gx', -1))  5.44 us
    pallas_call x1, Pallas kernels, inner_sums(): kernel_call(inner_kernel, [((8 * 9 * S, 2 * S), BF16), ((8 * 9 * S, 2 * S...  4.84 us
    ppermute x1, starting transfers between devices, per_device(): below = lax.ppermute(rows[:, 1:2], 'gy', ring('gy', 1))  3.85 us
    ppermute x1, waiting for transfers between devices, per_device(): above = lax.ppermute(rows[:, 0:1], 'gy', ring('gy', -1))  3.56 us
    ppermute x1, starting transfers between devices, per_device(): behind = lax.ppermute(cells[:, :, 7:8], 'gz', ring('gz', 1))  3.48 us
    pallas_call x1, Pallas kernels, plane_sums(): kernel_call(plane_kernel, [((4, CELLS, S), F32), FAR, FAR, OWN_BLOCKS], [...  2.96 us
  transfers between devices with their start and end apart: 6, of which 2 were waited for; matrix products, arithmetic and copies ran while one was open for 0% of the time, Pallas kernels for 9%

profile of v4, /device:TPU:6, one launch (start us, length us, event | category | flops | bytes accessed | tf_op | source)
XLA Modules:
  0.0 67.7 jit_solution(1345293685993436533)
XLA Ops:
  0.6 1.4 %sort.1 = (f32[3,16,128]{2,1,0:T(8,128)S(1)}, f32[16,128]{1,0:T(8,128)S(1)}) custom-call(f32[3,1,2,8,128]{4,3,2,1,0:T(8,128)} %pos_hbm.1, s32[1,2,8]{2,1,0:T(2,128)} %counts_hbm.1), custom_call_target="tpu_custom_call" | custom-call | tf_op jit(solution)/shard_map/sort/pallas_call | solution.py:568
  2.1 3.5 %collective-permute-start = (f32[3,2,1,128]{3,2,1,0:T(1,128)S(1)}, f32[3,2,1,128]{3,2,1,0:T(1,128)S(1)}, u32[]{:S(2)}, u32[]{:S(2)}) collective-permute-start(f32[3,2,1,128]{3,2,1,0:T(1,128)S(1)} %get-tuple-element.38), channel_id=1, source_target_pairs={{0,32},{32,64},{64,96},{96,128},{128,160},{160,192},{192,224},{224... | collective-permute-start | bytes 9224 | tf_op jit(solution)/shard_map/ppermute | solution.py:640
  5.6 19.5 %collective-permute-start.1 = (f32[3,2,1,128]{3,2,1,0:T(1,128)S(1)}, f32[3,2,1,128]{3,2,1,0:T(1,128)S(1)}, u32[]{:S(2)}, u32[]{:S(2)}) collective-permute-start(f32[3,2,1,128]{3,2,1,0:T(1,128)S(1)} %get-tuple-element.39), channel_id=1, source_target_pairs={{0,992},{32,0},{64,32},{96,64},{128,96},{160,128},{192,160},{224,1... | collective-permute-start | bytes 9224 | tf_op jit(solution)/shard_map/ppermute | solution.py:641
  25.1 0.0 collective-permute-done
  25.1 1.3 %collective-permute-done.1 = f32[3,2,1,128]{3,2,1,0:T(1,128)S(1)} collective-permute-done((f32[3,2,1,128]{3,2,1,0:T(1,128)S(1)}, f32[3,2,1,128]{3,2,1,0:T(1,128)S(1)}, u32[]{:S(2)}, u32[]{:S(2)}) %collective-permute-start.1) | collective-permute-done | bytes 3104 | tf_op jit(solution)/shard_map/ppermute | solution.py:641
  26.4 3.8 %collective-permute-start.2 = (f32[3,1,10,128]{3,2,1,0:T(8,128)S(1)}, f32[3,1,10,128]{3,2,1,0:T(8,128)S(1)}, u32[]{:S(2)}, u32[]{:S(2)}) collective-permute-start(f32[3,1,10,128]{3,2,1,0:T(8,128)S(1)} %get-tuple-element.37), channel_id=1, source_target_pairs={{0,8},{8,16},{16,24},{24,0},{1,9},{9,17},{17,25},{25,1},{2,10},{10... | collective-permute-start | bytes 46088 | tf_op jit(solution)/shard_map/ppermute | solution.py:643
  30.3 2.0 %collective-permute-start.3 = (f32[3,1,10,128]{3,2,1,0:T(8,128)S(1)}, f32[3,1,10,128]{3,2,1,0:T(8,128)S(1)}, u32[]{:S(2)}, u32[]{:S(2)}) collective-permute-start(f32[3,1,10,128]{3,2,1,0:T(8,128)S(1)} %get-tuple-element.36), channel_id=1, source_target_pairs={{0,24},{8,0},{16,8},{24,16},{1,25},{9,1},{17,9},{25,17},{2,26},{10... | collective-permute-start | bytes 46088 | tf_op jit(solution)/shard_map/ppermute | solution.py:644
  32.3 1.4 %rows.1 = (bf16[1536,64]{1,0:T(8,128)(2,1)S(1)}, bf16[2,768,256]{2,1,0:T(8,128)(2,1)S(1)}, f32[10,256]{1,0:T(8,128)S(1)}) custom-call(f32[3,2,10,128]{3,2,1,0:T(8,128)S(1)} %pad_maximum_fusion.pos_ref), custom_call_target="tpu_custom_call" | custom-call | tf_op jit(solution)/shard_map/rows/pallas_call | solution.py:584
  33.7 0.0 collective-permute-done.2.below_ref
  33.7 3.6 %collective-permute-done.3.above_ref = f32[3,1,10,128]{3,2,1,0:T(8,128)S(1)} collective-permute-done((f32[3,1,10,128]{3,2,1,0:T(8,128)S(1)}, f32[3,1,10,128]{3,2,1,0:T(8,128)S(1)}, u32[]{:S(2)}, u32[]{:S(2)}) %collective-permute-start.3) | collective-permute-done | bytes 15392 | tf_op jit(solution)/shard_map/ppermute | solution.py:644
  37.2 3.0 %plane.1 = (f32[4,40,128]{2,1,0:T(8,128)S(1)}, bf16[1536,64]{1,0:T(8,128)(2,1)S(1)}, bf16[1536,64]{1,0:T(8,128)(2,1)S(1)}, bf16[2,768,256]{2,1,0:T(8,128)(2,1)S(1)}) custom-call(f32[3,2,10,128]{3,2,1,0:T(8,128)S(1)} %pad_maximum_fusion.pos_ref, f32[3,1,10,128]{3,2,1,0:T(8,128)S(1)} %collective-permute-done.2.below_ref, ...), custom_call_target="tpu_custom_call" | custom-call | tf_op jit(solution)/shard_map/plane/pallas_call | solution.py:593
  40.2 1.9 %collective-permute-start.4 = (f32[4,40,128]{2,1,0:T(8,128)S(1)}, f32[4,40,128]{2,1,0:T(8,128)S(1)}, u32[]{:S(2)}, u32[]{:S(2)}) collective-permute-start(f32[4,40,128]{2,1,0:T(8,128)S(1)} %get-tuple-element.22.plane_ref), channel_id=1, source_target_pairs={{0,1},{1,2},{2,3},{3,4},{4,5},{5,6},{6,7},{7,0},{8,9},{9,10},{10,1... | collective-permute-start | bytes 245768 | tf_op jit(solution)/shard_map/ppermute | solution.py:647
  42.1 5.4 %collective-permute-start.5 = (f32[4,40,128]{2,1,0:T(8,128)S(1)}, f32[4,40,128]{2,1,0:T(8,128)S(1)}, u32[]{:S(2)}, u32[]{:S(2)}) collective-permute-start(f32[4,40,128]{2,1,0:T(8,128)S(1)} %get-tuple-element.22.plane_ref), channel_id=1, source_target_pairs={{0,7},{1,0},{2,1},{3,2},{4,3},{5,4},{6,5},{7,6},{8,15},{9,8},{10,9... | collective-permute-start | bytes 245768 | tf_op jit(solution)/shard_map/ppermute | solution.py:648
  47.6 4.8 %inner.1 = (bf16[9216,256]{1,0:T(8,128)(2,1)S(1)}, bf16[9216,256]{1,0:T(8,128)(2,1)S(1)}, f32[64,128]{1,0:T(8,128)S(1)}, f32[16,128]{1,0:T(8,128)S(1)}, bf16[3,160,128]{2,1,0:T(8,128)(2,1)S(1)}) custom-call(f32[4,40,128]{2,1,0:T(8,128)S(1)} %get-tuple-element.22.plane_ref, bf16[1536,64]{1,0:T(8,128)(2,1)S(1)} %get-tuple-element.19.mid_ref, ...), custom_call_target="tpu_custom_call" | custom-call | tf_op jit(solution)/shard_map/inner/pallas_call | solution.py:602
  52.4 0.0 collective-permute-done.4.low_ref
  52.4 0.0 collective-permute-done.5.high_ref
  52.5 15.3 %forces.1 = (f32[16,128]{1,0:T(8,128)}, f32[48,128]{1,0:T(8,128)}) custom-call(f32[4,40,128]{2,1,0:T(8,128)S(1)} %get-tuple-element.22.plane_ref, f32[4,40,128]{2,1,0:T(8,128)S(1)} %collective-permute-done.4.low_ref, f32[4,40,128]{2,1,0:T(8,128)S(1)} %collective-permute-done.5.high_ref, bf16[2,768,256]{2,1,0:T(8,128)(2,1)S(1)} %get-tuple-element.20.own_ref, ...), custom_call_target="tpu_custom_call" | custom-call | tf_op jit(solution)/shard_map/forces/pallas_call | solution.py:617
  (3 shorter events, 0.0 us)
Async XLA Ops:
  2.1 23.0 %collective-permute-start = (f32[3,2,1,128]{3,2,1,0:T(1,128)S(1)}, f32[3,2,1,128]{3,2,1,0:T(1,128)S(1)}, u32[]{:S(2)}, u32[]{:S(2)}) collective-permute-start(f32[3,2,1,128]{3,2,1,0:T(1,128)S(1)} %get-tuple-element.38), channel_id=1, source_target_pairs={{0,32},{32,64},{64,96},{96,128},{128,160},{160,192},{192,224},{224... | collective-permute-start | bytes 9224 | tf_op jit(solution)/shard_map/ppermute | solution.py:640
  5.6 20.8 %collective-permute-start.1 = (f32[3,2,1,128]{3,2,1,0:T(1,128)S(1)}, f32[3,2,1,128]{3,2,1,0:T(1,128)S(1)}, u32[]{:S(2)}, u32[]{:S(2)}) collective-permute-start(f32[3,2,1,128]{3,2,1,0:T(1,128)S(1)} %get-tuple-element.39), channel_id=1, source_target_pairs={{0,992},{32,0},{64,32},{96,64},{128,96},{160,128},{192,160},{224,1... | collective-permute-start | bytes 9224 | tf_op jit(solution)/shard_map/ppermute | solution.py:641
  26.4 7.2 %collective-permute-start.2 = (f32[3,1,10,128]{3,2,1,0:T(8,128)S(1)}, f32[3,1,10,128]{3,2,1,0:T(8,128)S(1)}, u32[]{:S(2)}, u32[]{:S(2)}) collective-permute-start(f32[3,1,10,128]{3,2,1,0:T(8,128)S(1)} %get-tuple-element.37), channel_id=1, source_target_pairs={{0,8},{8,16},{16,24},{24,0},{1,9},{9,17},{17,25},{25,1},{2,10},{10... | collective-permute-start | bytes 46088 | tf_op jit(solution)/shard_map/ppermute | solution.py:643
  30.3 6.9 %collective-permute-start.3 = (f32[3,1,10,128]{3,2,1,0:T(8,128)S(1)}, f32[3,1,10,128]{3,2,1,0:T(8,128)S(1)}, u32[]{:S(2)}, u32[]{:S(2)}) collective-permute-start(f32[3,1,10,128]{3,2,1,0:T(8,128)S(1)} %get-tuple-element.36), channel_id=1, source_target_pairs={{0,24},{8,0},{16,8},{24,16},{1,25},{9,1},{17,9},{25,17},{2,26},{10... | collective-permute-start | bytes 46088 | tf_op jit(solution)/shard_map/ppermute | solution.py:644
  40.2 12.2 %collective-permute-start.4 = (f32[4,40,128]{2,1,0:T(8,128)S(1)}, f32[4,40,128]{2,1,0:T(8,128)S(1)}, u32[]{:S(2)}, u32[]{:S(2)}) collective-permute-start(f32[4,40,128]{2,1,0:T(8,128)S(1)} %get-tuple-element.22.plane_ref), channel_id=1, source_target_pairs={{0,1},{1,2},{2,3},{3,4},{4,5},{5,6},{6,7},{7,0},{8,9},{9,10},{10,1... | collective-permute-start | bytes 245768 | tf_op jit(solution)/shard_map/ppermute | solution.py:647
  42.1 10.3 %collective-permute-start.5 = (f32[4,40,128]{2,1,0:T(8,128)S(1)}, f32[4,40,128]{2,1,0:T(8,128)S(1)}, u32[]{:S(2)}, u32[]{:S(2)}) collective-permute-start(f32[4,40,128]{2,1,0:T(8,128)S(1)} %get-tuple-element.22.plane_ref), channel_id=1, source_target_pairs={{0,7},{1,0},{2,1},{3,2},{4,3},{5,4},{6,5},{7,6},{8,15},{9,8},{10,9... | collective-permute-start | bytes 245768 | tf_op jit(solution)/shard_map/ppermute | solution.py:648
